TPU v7x, 32 devices: a whole 2x2x4 slice. The times are simulated.
32 devices in a mesh: dp: 16 (over z, x, core), seq: 2 (over y).
Axes of the slice: x: 2, y: 2, z: 4, core: 2. Of those that a mesh axis runs over, the one named last changes fastest.
Arguments:
- tokens: float32 [16384, 1024], P(('dp', 'seq')), may hold values from -6 to 6
- lengths: int32 [16, 1], P('dp'), may hold values from 1024 to 1024, as said below
- attn_gain: bfloat16 [1024], P('dp'), may hold values from 0.5 to 1.5
- w_query: bfloat16 [1024, 1024], P('dp'), may hold values from -0.1875 to 0.1875
- w_key: bfloat16 [1024, 512], P('dp'), may hold values from -0.1875 to 0.1875
- w_value: bfloat16 [1024, 512], P('dp'), may hold values from -0.1875 to 0.1875
- query_gain: bfloat16 [64], P('dp'), may hold values from 1 to 2
- key_gain: bfloat16 [64], P('dp'), may hold values from 0.5 to 1.5
- w_out: bfloat16 [1024, 1024], P('dp'), may hold values from -1.5 to 1.5
- ffn_gain: bfloat16 [1024], P('dp'), may hold values from 0.5 to 1.5
- w_gate: bfloat16 [1024, 4608], P('dp'), may hold values from -0.1875 to 0.1875
- w_up: bfloat16 [1024, 4608], P('dp'), may hold values from -0.1875 to 0.1875
- w_down: bfloat16 [4608, 1024], P('dp'), may hold values from -0.09375 to 0.09375
- cotangent: float32 [16384, 1024], P(('dp', 'seq')), may hold values from -6 to 6
Outputs:
- block_out: float32 [16384, 1024], P(('dp', 'seq'))
- d_tokens: float32 [16384, 1024], P(('dp', 'seq'))
- d_attn_gain: float32 [1024], P('dp')
- d_w_query: float32 [1024, 1024], P('dp')
- d_w_key: float32 [1024, 512], P('dp')
- d_w_value: float32 [1024, 512], P('dp')
- d_query_gain: float32 [64], P('dp')
- d_key_gain: float32 [64], P('dp')
- d_w_out: float32 [1024, 1024], P('dp')
- d_ffn_gain: float32 [1024], P('dp')
- d_w_gate: float32 [1024, 4608], P('dp')
- d_w_up: float32 [1024, 4608], P('dp')
- d_w_down: float32 [4608, 1024], P('dp')
Inputs may be any that keep to these rules, and one draw needn't show every extreme that they name: `lengths`: every length is at least 1024; in every draw one pack, drawn from the seed, has every sequence of length 1024 and no padding.
All inputs are finite; a program needn't handle non-finite values.
Results may differ from a plain program's by a relative error of at most 0.02.
Values may be sent and summed in bfloat16 or wider, within the bound.
No kernel may reach another device: no remote copies, remote signals or barrier semaphores. Data moves between devices by JAX's collectives and lax.ppermute only.
A program may use at most 192 MiB of HBM per device.

v0:
```python
from functools import partial
import math

import jax
import jax.numpy as jnp
from jax import lax
from jax.sharding import PartitionSpec as P

H = 16
KV = 8
HD = 64


EPSILON = 1e-05
ROPE_BASE = 1000000.0
MASKED_SCORE = -1e30


def rms_norm(values, gain_vec):
    return (
        values * lax.rsqrt(jnp.mean(values * values, axis=-1, keepdims=True) + EPSILON) * gain_vec
    )


def rope_tables(positions, head_size):
    half_size = head_size // 2
    freqs = ROPE_BASE ** (-(jnp.arange(half_size, dtype=jnp.float32) * (2.0 / head_size)))
    angles = positions.astype(jnp.float32)[:, None] * freqs[None, :]
    return (jnp.cos(angles), jnp.sin(angles))


def rotate(values, cos_tab, sin_tab):
    half_size = values.shape[-1] // 2
    first = values[..., :half_size]
    second = values[..., half_size:]
    cos_b = cos_tab[:, None, :]
    sin_b = sin_tab[:, None, :]
    return jnp.concatenate(
        [first * cos_b - second * sin_b, second * cos_b + first * sin_b], axis=-1
    )


def qk_prep(linear, gain_vec, cos_tab, sin_tab, heads):
    shaped = linear.reshape(linear.shape[0], heads, -1)
    return rotate(rms_norm(shaped, gain_vec), cos_tab, sin_tab)


def swiglu(gate_act, up_act):
    return jax.nn.silu(gate_act) * up_act


def pack_layout(seq_lens, total):
    places = jnp.arange(total, dtype=jnp.int32)
    ends = jnp.cumsum(seq_lens)
    starts = ends - seq_lens
    segment = jnp.sum((places[:, None] >= ends[None, :]).astype(jnp.int32), axis=1)
    starts_ext = jnp.concatenate([starts, ends[-1:]])
    labels = jnp.arange(seq_lens.shape[0] + 1, dtype=jnp.int32)
    offset = jnp.sum(jnp.where(segment[:, None] == labels[None, :], starts_ext[None, :], 0), axis=1)
    return (places, segment, places - offset, segment < seq_lens.shape[0])


def mat_dot(form, left, right):
    return jnp.einsum(form, left, right, preferred_element_type=jnp.float32)


def body(
    tokens,
    lengths,
    attn_gain,
    w_query,
    w_key,
    w_value,
    query_gain,
    key_gain,
    w_out,
    ffn_gain,
    w_gate,
    w_up,
    w_down,
    cotangent,
):
    seq_count = lax.axis_size("seq")
    seq_rank = lax.axis_index("seq")
    tok_rows = tokens.shape[0]
    pack_len = tok_rows * seq_count
    local_kv = KV // seq_count
    group = H // KV
    local_q = local_kv * group
    score_scale = 1.0 / math.sqrt(HD)
    blk_rows = min(512, pack_len)
    blocks = pack_len // blk_rows
    places, segment, positions, valid = pack_layout(lengths[0], pack_len)
    first_row = seq_rank * tok_rows
    my_pos = lax.dynamic_slice_in_dim(positions, first_row, tok_rows)
    my_valid = lax.dynamic_slice_in_dim(valid, first_row, tok_rows).astype(jnp.float32)[:, None]
    gain_attn, query_full, key_full, value_full, gain_query, gain_key, out_full = (
        lax.all_gather(attn_gain, "dp", axis=0, tiled=True),
        lax.all_gather(w_query, "dp", axis=0, tiled=True),
        lax.all_gather(w_key, "dp", axis=0, tiled=True),
        lax.all_gather(w_value, "dp", axis=0, tiled=True),
        lax.all_gather(query_gain, "dp", axis=0, tiled=True),
        lax.all_gather(key_gain, "dp", axis=0, tiled=True),
        lax.all_gather(w_out, "dp", axis=0, tiled=True),
    )
    gain_ffn, gate_full, up_full, down_full = (
        lax.all_gather(ffn_gain, "dp", axis=0, tiled=True),
        lax.all_gather(w_gate, "dp", axis=0, tiled=True),
        lax.all_gather(w_up, "dp", axis=0, tiled=True),
        lax.all_gather(w_down, "dp", axis=0, tiled=True),
    )
    normed, pull_attn_norm = jax.vjp(rms_norm, tokens, gain_attn.astype(jnp.float32))
    normed_low = normed.astype(jnp.bfloat16)
    q_lin = jnp.dot(normed_low, query_full, preferred_element_type=jnp.float32)
    k_lin = jnp.dot(normed_low, key_full, preferred_element_type=jnp.float32)
    v_lin = jnp.dot(normed_low, value_full, preferred_element_type=jnp.float32)
    cos_tab, sin_tab = rope_tables(my_pos, HD)
    queries, pull_query = jax.vjp(
        partial(qk_prep, cos_tab=cos_tab, sin_tab=sin_tab, heads=H),
        q_lin,
        gain_query.astype(jnp.float32),
    )
    key_rows, pull_key = jax.vjp(
        partial(qk_prep, cos_tab=cos_tab, sin_tab=sin_tab, heads=KV),
        k_lin,
        gain_key.astype(jnp.float32),
    )
    q_heads, k_heads, v_heads = (
        lax.all_to_all(
            queries.astype(jnp.bfloat16).reshape(tok_rows, seq_count, -1),
            "seq",
            split_axis=1,
            concat_axis=0,
            tiled=True,
        ),
        lax.all_to_all(
            key_rows.astype(jnp.bfloat16).reshape(tok_rows, seq_count, -1),
            "seq",
            split_axis=1,
            concat_axis=0,
            tiled=True,
        ),
        lax.all_to_all(
            v_lin.astype(jnp.bfloat16).reshape(tok_rows, seq_count, -1),
            "seq",
            split_axis=1,
            concat_axis=0,
            tiled=True,
        ),
    )
    query_blocks = q_heads.reshape(blocks, blk_rows, local_kv, group, HD)
    key_all = k_heads.reshape(pack_len, local_kv, HD)
    value_all = v_heads.reshape(pack_len, local_kv, HD)
    seg_blocks = segment.reshape(blocks, blk_rows)
    place_blocks = places.reshape(blocks, blk_rows)

    def scores_of(query_blk, seg_blk, place_blk):
        scores = mat_dot("qkgd,skd->kgqs", query_blk, key_all) * score_scale
        allowed = (seg_blk[:, None] == segment[None, :]) & (places[None, :] <= place_blk[:, None])
        return jnp.where(allowed[None, None], scores, MASKED_SCORE)

    def forward_block(inputs):
        query_blk, seg_blk, place_blk = inputs
        scores = scores_of(query_blk, seg_blk, place_blk)
        top_val = jnp.max(scores, axis=-1, keepdims=True)
        expo = jnp.exp(scores - top_val)
        total = jnp.sum(expo, axis=-1, keepdims=True)
        probs = (expo / total).astype(jnp.bfloat16)
        attended_blk = mat_dot("kgqs,skd->qkgd", probs, value_all)
        return (attended_blk, (top_val + jnp.log(total))[..., 0])

    attended_heads, log_sums = lax.map(forward_block, (query_blocks, seg_blocks, place_blocks))
    attended_send = attended_heads.reshape(pack_len, 1, local_q * HD).astype(jnp.bfloat16)
    attended = lax.all_to_all(
        attended_send, "seq", split_axis=0, concat_axis=1, tiled=True
    ).reshape(tok_rows, -1)
    resid = tokens + jnp.dot(attended, out_full, preferred_element_type=jnp.float32)
    ffn_in, pull_ffn_norm = jax.vjp(rms_norm, resid, gain_ffn.astype(jnp.float32))
    ffn_low = ffn_in.astype(jnp.bfloat16)
    gate_act = jnp.dot(ffn_low, gate_full, preferred_element_type=jnp.float32)
    up_act = jnp.dot(ffn_low, up_full, preferred_element_type=jnp.float32)
    hidden, pull_swiglu = jax.vjp(swiglu, gate_act, up_act)
    hidden_low = hidden.astype(jnp.bfloat16)
    block_out = (
        resid + jnp.dot(hidden_low, down_full, preferred_element_type=jnp.float32)
    ) * my_valid
    query_back, key_back, value_back, out_back = (
        lax.all_gather(w_query, "dp", axis=0, tiled=True),
        lax.all_gather(w_key, "dp", axis=0, tiled=True),
        lax.all_gather(w_value, "dp", axis=0, tiled=True),
        lax.all_gather(w_out, "dp", axis=0, tiled=True),
    )
    gate_back, up_back, down_back = (
        lax.all_gather(w_gate, "dp", axis=0, tiled=True),
        lax.all_gather(w_up, "dp", axis=0, tiled=True),
        lax.all_gather(w_down, "dp", axis=0, tiled=True),
    )
    grad = cotangent * my_valid
    grad_low = grad.astype(jnp.bfloat16)
    d_down = mat_dot("tf,td->fd", hidden_low, grad_low)
    d_hidden = mat_dot("td,fd->tf", grad_low, down_back)
    d_gate, d_up = pull_swiglu(d_hidden)
    d_gate_low = d_gate.astype(jnp.bfloat16)
    d_up_low = d_up.astype(jnp.bfloat16)
    d_gate_w = mat_dot("td,tf->df", ffn_low, d_gate_low)
    d_up_w = mat_dot("td,tf->df", ffn_low, d_up_low)
    d_ffn = mat_dot("tf,df->td", d_gate_low, gate_back) + mat_dot("tf,df->td", d_up_low, up_back)
    d_resid_norm, d_gain_ffn = pull_ffn_norm(d_ffn)
    ffn_shards = (
        lax.psum_scatter(d_gain_ffn, "dp", scatter_dimension=0, tiled=True),
        lax.psum_scatter(d_gate_w, "dp", scatter_dimension=0, tiled=True),
        lax.psum_scatter(d_up_w, "dp", scatter_dimension=0, tiled=True),
        lax.psum_scatter(d_down, "dp", scatter_dimension=0, tiled=True),
    )
    d_resid = grad + d_resid_norm
    resid_low = d_resid.astype(jnp.bfloat16)
    d_out_w = mat_dot("tq,td->qd", attended, resid_low)
    d_attended = mat_dot("td,qd->tq", resid_low, out_back).astype(jnp.bfloat16)
    d_att_heads = lax.all_to_all(
        d_attended.reshape(tok_rows, seq_count, -1), "seq", split_axis=1, concat_axis=0, tiled=True
    )
    d_att_blocks = d_att_heads.reshape(blocks, blk_rows, local_kv, group, HD)

    def backward_block(carry, inputs):
        d_key_acc, d_value_acc = carry
        query_blk, seg_blk, place_blk, log_sum, d_att_blk = inputs
        scores = scores_of(query_blk, seg_blk, place_blk)
        probs = jnp.exp(scores - log_sum[..., None])
        d_value_acc = d_value_acc + mat_dot("kgqs,qkgd->skd", probs.astype(jnp.bfloat16), d_att_blk)
        d_probs = mat_dot("qkgd,skd->kgqs", d_att_blk, value_all)
        delta = jnp.sum(probs * d_probs, axis=-1, keepdims=True)
        d_scores = (probs * (d_probs - delta)).astype(jnp.bfloat16)
        d_query_blk = mat_dot("kgqs,skd->qkgd", d_scores, key_all) * score_scale
        d_key_acc = d_key_acc + mat_dot("kgqs,qkgd->skd", d_scores, query_blk) * score_scale
        return ((d_key_acc, d_value_acc), d_query_blk)

    zero_kv = jnp.zeros((pack_len, local_kv, HD), jnp.float32)
    (d_key_all, d_value_all), d_query_all = lax.scan(
        backward_block,
        (zero_kv, zero_kv),
        (query_blocks, seg_blocks, place_blocks, log_sums, d_att_blocks),
    )
    d_q_tok, d_k_tok, d_v_tok = (
        lax.all_to_all(
            d_query_all.reshape(pack_len, 1, -1).astype(jnp.bfloat16),
            "seq",
            split_axis=0,
            concat_axis=1,
            tiled=True,
        ),
        lax.all_to_all(
            d_key_all.reshape(pack_len, 1, -1).astype(jnp.bfloat16),
            "seq",
            split_axis=0,
            concat_axis=1,
            tiled=True,
        ),
        lax.all_to_all(
            d_value_all.reshape(pack_len, 1, -1).astype(jnp.bfloat16),
            "seq",
            split_axis=0,
            concat_axis=1,
            tiled=True,
        ),
    )
    d_q_lin, d_gain_query = pull_query(d_q_tok.reshape(tok_rows, H, HD).astype(jnp.float32))
    d_k_lin, d_gain_key = pull_key(d_k_tok.reshape(tok_rows, KV, HD).astype(jnp.float32))
    d_q_low = d_q_lin.astype(jnp.bfloat16)
    d_k_low = d_k_lin.astype(jnp.bfloat16)
    d_v_low = d_v_tok.reshape(tok_rows, -1)
    d_query_w = mat_dot("td,tq->dq", normed_low, d_q_low)
    d_key_w = mat_dot("td,tq->dq", normed_low, d_k_low)
    d_value_w = mat_dot("td,tq->dq", normed_low, d_v_low)
    d_normed = (
        mat_dot("tq,dq->td", d_q_low, query_back)
        + mat_dot("tq,dq->td", d_k_low, key_back)
        + mat_dot("tq,dq->td", d_v_low, value_back)
    )
    d_tok_norm, d_gain_attn = pull_attn_norm(d_normed)
    d_tokens = d_resid + d_tok_norm
    attn_shards = (
        lax.psum_scatter(d_gain_attn, "dp", scatter_dimension=0, tiled=True),
        lax.psum_scatter(d_query_w, "dp", scatter_dimension=0, tiled=True),
        lax.psum_scatter(d_key_w, "dp", scatter_dimension=0, tiled=True),
        lax.psum_scatter(d_value_w, "dp", scatter_dimension=0, tiled=True),
        lax.psum_scatter(d_gain_query, "dp", scatter_dimension=0, tiled=True),
        lax.psum_scatter(d_gain_key, "dp", scatter_dimension=0, tiled=True),
        lax.psum_scatter(d_out_w, "dp", scatter_dimension=0, tiled=True),
    )
    summed = lax.psum(
        (
            attn_shards[0],
            attn_shards[1],
            attn_shards[2],
            attn_shards[3],
            attn_shards[4],
            attn_shards[5],
            attn_shards[6],
            ffn_shards[0],
            ffn_shards[1],
            ffn_shards[2],
            ffn_shards[3],
        ),
        "seq",
    )
    return (
        block_out,
        d_tokens,
        summed[0],
        summed[1],
        summed[2],
        summed[3],
        summed[4],
        summed[5],
        summed[6],
        summed[7],
        summed[8],
        summed[9],
        summed[10],
    )


def solution(mesh):
    return jax.shard_map(
        body,
        mesh=mesh,
        in_specs=(
            P(("dp", "seq"), None),
            P("dp", None),
            P("dp"),
            P("dp", None),
            P("dp", None),
            P("dp", None),
            P("dp"),
            P("dp"),
            P("dp", None),
            P("dp"),
            P("dp", None),
            P("dp", None),
            P("dp", None),
            P(("dp", "seq"), None),
        ),
        out_specs=(
            P(("dp", "seq"), None),
            P(("dp", "seq"), None),
            P("dp"),
            P("dp", None),
            P("dp", None),
            P("dp", None),
            P("dp"),
            P("dp"),
            P("dp", None),
            P("dp"),
            P("dp", None),
            P("dp", None),
            P("dp", None),
        ),
        check_vma=False,
    )
```

profile of v0, /device:TPU:0, one launch (start us, length us, event | category | flops | bytes accessed | tf_op | source)
XLA Modules:
  0.0 1585.9 jit_solution(17672986321578510262)
XLA Ops:
  15.5 36.1 %all-reduce.16 = (bf16[64]{0:T(256)(128)(2,1)S(1)}, bf16[1024]{0:T(1024)(128)(2,1)S(1)}, bf16[64]{0:T(256)(128)(2,1)S(1)}, bf16[1024]{0:T(1024)(128)(2,1)}) all-reduce(bf16[64]{0:T(256)(128)(2,1)S(1)} %dynamic-update-slice.1, bf16[1024]{0:T(1024)(128)(2,1)S(1)} %dynamic-update-slice, ...), channel_id=1, replica_groups=mesh['dp'=16,'seq'=2] {'dp'}, use_global_device_ids=true, to_apply=%add.6 | all-reduce | flops 2176 | bytes 8704
  57.2 4.2 all-to-all-start.1
  61.4 28.7 %all-gather.12.cloned.1.call-done = bf16[1024,512]{1,0:T(8,128)(2,1)} async-done(((bf16[64,512]{1,0:T(8,128)(2,1)}), bf16[1024,512]{1,0:T(8,128)(2,1)}) %all-gather.12.cloned.1.call-update) | async-done | bytes 1048592 | tf_op jit(solution)/shard_map/all_gather | solution.py:101
  92.9 39.9 %all-gather.8.cloned.1.call-done = bf16[1024,1024]{1,0:T(8,128)(2,1)} async-done(((bf16[64,1024]{1,0:T(8,128)(2,1)}), bf16[1024,1024]{1,0:T(8,128)(2,1)}) %all-gather.8.cloned.1.call-update) | async-done | bytes 2097168 | tf_op jit(solution)/shard_map/all_gather | solution.py:99
  137.5 3.5 all-to-all-start.2
  142.4 7.2 all-to-all-done.2
  149.6 4.6 all-to-all-start
  157.2 10.7 all-to-all-done
  167.9 29.5 %while.28 = (s32[]{:T(128)}, bf16[2,512,4,2,64]{1,4,3,2,0:T(8,128)(2,1)S(1)}, f32[2,4,2,512]{3,2,1,0:T(2,128)S(1)}, s32[2,512]{1,0:T(2,128)S(1)}, s32[2,512]{1,0...) while((s32[]{:T(128)}, ...), condition=%wide.region_7.8_spmd.clone, body=%wide.region_4.7_spmd.clone.sunk | while | flops 1125644288 | bytes 55201920 | solution.py:172
  169.2 3.9 bitcast_reduce_fusion.2
  173.2 4.3 fusion.152
  177.5 5.2 fusion.153
  184.0 4.0 bitcast_reduce_fusion.2
  187.9 4.3 fusion.152
  192.2 5.2 fusion.153
  198.1 3.8 copy.125
  201.9 7.7 reshape.486
  210.1 8.0 reduce
  220.8 3.6 all-to-all-start.3
  224.5 12.6 all-to-all-done.3
  239.4 3.3 copy.129
  249.8 6.9 all-gather.16.cloned.1.call-done
  256.8 11.0 fusion.78
  267.8 70.4 %all-gather.18.cloned.1.call-done = bf16[1024,4608]{1,0:T(8,128)(2,1)} async-done(((bf16[64,4608]{1,0:T(8,128)(2,1)}), bf16[1024,4608]{1,0:T(8,128)(2,1)}) %all-gather.18.cloned.1.call-update) | async-done | bytes 9437200 | tf_op jit(solution)/shard_map/all_gather | solution.py:109
  338.3 11.1 fusion.79
  349.4 70.5 %all-gather.20.cloned.1.call-done = bf16[4608,1024]{1,0:T(8,128)(2,1)} async-done(((bf16[288,1024]{1,0:T(8,128)(2,1)}), bf16[4608,1024]{1,0:T(8,128)(2,1)}) %all-gather.20.cloned.1.call-update) | async-done | bytes 9437200 | tf_op jit(solution)/shard_map/all_gather | solution.py:110
  419.9 18.5 %multiply_convert_fusion = (bf16[512,4608]{1,0:T(8,128)(2,1)}, bf16[512,4608]{1,0:T(8,128)(2,1)}, bf16[512,4608]{1,0:T(8,128)(2,1)}) fusion(f32[512,4608]{1,0:T(8,128)} %fusion.78, f32[512,4608]{1,0:T(8,128)} %fusion.79, bf16[4608,1024]{1,0:T(8,128)(2,1)} %all-gather.20.cloned.1.call-done, f32[512,1024]{1,0:T(8,128)} %param.31, ...), kind=kOutput, calls=%fused_computation.73 | convolution fusion | flops 4870635520 | bytes 44566528 | tf_op jit(solution)/shard_map/td,fd->tf/dot_general | solution.py:64
  438.4 9.2 fusion.80
  447.6 8.9 multiply_reduce_fusion
  460.5 3.6 all-to-all-start.4
  464.1 14.2 all-to-all-done.4
  480.7 87.6 %while.29 = (s32[]{:T(128)}, f32[1024,4,64]{0,2,1:T(8,128)}, f32[1024,4,64]{0,2,1:T(8,128)}, bf16[2,512,4,2,64]{1,4,3,2,0:T(8,128)(2,1)}, bf16[2,512,4,2,64]{1,4...) while((s32[]{:T(128)}, f32[1024,4,64]{0,2,1:T(8,128)}, ...), condition=%wide.region_12.13_spmd.clone, body=%wide.region_10.12_spmd.clone.sunk | while | flops 2725246976 | bytes 186356192 | solution.py:238
  480.7 3.6 fusion.162
  486.3 11.2 fusion.165
  497.4 9.4 fusion.166
  506.8 6.2 fusion.167
  513.1 7.6 fusion.168
  524.4 3.6 fusion.162
  530.0 11.2 fusion.165
  541.1 9.4 fusion.166
  550.5 6.5 fusion.167
  557.0 7.6 fusion.168
  571.1 10.4 all_to_all.108
  590.1 9.4 all_to_all.109
  604.5 4.5 fusion.66
  610.2 4.2 copy.126
  614.4 7.5 reshape.487
  621.8 8.0 reduce.2
  631.7 15.2 all_to_all.110
  656.8 3.3 fusion.83
  661.3 11.6 fusion.86
  673.0 11.5 fusion.87
  686.1 11.6 fusion.75
  698.0 14.5 reduce-scatter.12.cloned.1.call-done
  712.5 75.5 %reduce-scatter.14.cloned.1.call-done = f32[64,1024]{1,0:T(8,128)} async-done(((f32[1024,1024]{1,0:T(8,128)}), f32[64,1024]{1,0:T(8,128)}) %reduce-scatter.14.cloned.1.call-update) | async-done | bytes 262160 | tf_op jit(solution)/shard_map/reduce_scatter | solution.py:288
  788.0 75.7 %reduce-scatter.8.cloned.1.call-done = f32[64,1024]{1,0:T(8,128)} async-done(((f32[1024,1024]{1,0:T(8,128)}), f32[64,1024]{1,0:T(8,128)}) %reduce-scatter.8.cloned.1.call-update) | async-done | bytes 262160 | tf_op jit(solution)/shard_map/reduce_scatter | solution.py:283
  863.7 197.0 %reduce-scatter.16.cloned.1.call-done = f32[64,4608]{1,0:T(8,128)} async-done(((f32[1024,4608]{1,0:T(8,128)}), f32[64,4608]{1,0:T(8,128)}) %reduce-scatter.16.cloned.1.call-update) | async-done | bytes 1179664 | tf_op jit(solution)/shard_map/reduce_scatter | solution.py:211
  1060.7 197.3 %reduce-scatter.18.cloned.1.call-done = f32[64,4608]{1,0:T(8,128)} async-done(((f32[1024,4608]{1,0:T(8,128)}), f32[64,4608]{1,0:T(8,128)}) %reduce-scatter.18.cloned.1.call-update) | async-done | bytes 1179664 | tf_op jit(solution)/shard_map/reduce_scatter | solution.py:212
  1258.0 197.1 %reduce-scatter.20.cloned.1.call-done = f32[288,1024]{1,0:T(8,128)} async-done(((f32[4608,1024]{1,0:T(8,128)}), f32[288,1024]{1,0:T(8,128)}) %reduce-scatter.20.cloned.1.call-update) | async-done | bytes 1179664 | tf_op jit(solution)/shard_map/reduce_scatter | solution.py:213
  1456.7 10.1 add_multiply_fusion
  1473.2 32.5 %all-reduce.13 = (f32[1024]{0:T(1024)S(1)}, f32[64]{0:T(128)S(1)}, f32[64]{0:T(128)S(1)}, f32[1024]{0:T(1024)S(1)}) all-reduce(f32[1024]{0:T(1024)S(1)} %get-tuple-element.220, f32[64]{0:T(128)S(1)} %get-tuple-element.222, f32[64]{0:T(128)S(1)} %get-tuple-element.224, ...), channel_id=2, replica_groups=mesh['dp'=16,'seq'=2] {'dp'}, use_global_device_ids=true, to_apply=%region_17.18.clone | all-reduce | flops 2176 | bytes 17408
  1506.0 5.5 all-reduce.14
  1511.5 4.1 fusion.64
  1515.6 52.5 %all-reduce.19.cloned.1.call-done = (f32[64,1024]{1,0:T(8,128)}, f32[64,512]{1,0:T(8,128)}, f32[64,512]{1,0:T(8,128)}, f32[64,1024]{1,0:T(8,128)}, f32[64,4608]{...) async-done(((f32[64,1024]{1,0:T(8,128)}, f32[64,512]{1,0:T(8,128)}, f32[64,512]{1,0:T(8,128)}, f32[64,1024]{1,0:T(8,128)}, f32[64,4608]{1,0:T(8,128)}, ...) | async-done | bytes 4325392 | tf_op jit(solution)/shard_map/psum | solution.py:290
  (325 shorter events, 106.5 us)
Async XLA Ops:
  7.2 5.5 copy-start.65
  7.2 7.4 copy-start.68
  7.2 7.6 copy-start.69
  7.2 7.9 copy-start.70
  7.2 8.1 copy-start.71
  7.2 44.5 %copy-start.4 = (f32[512,1024]{1,0:T(8,128)S(1)}, f32[512,1024]{1,0:T(8,128)}, u32[]{:S(2)}) copy-start(f32[512,1024]{1,0:T(8,128)} %param.18) | copy-start | bytes 6291460
  7.2 46.0 %all-gather.10.cloned.1.call-start = ((), (), s32[]{:S(2)}) async-start(), calls=%async_computation.16 | async-start | bytes 1114112 | tf_op jit(solution)/shard_map/all_gather | solution.py:100
  8.0 82.2 %all-gather.12.cloned.1.call-start = ((), (), s32[]{:S(2)}) async-start(), calls=%async_computation.17 | async-start | bytes 1114112 | tf_op jit(solution)/shard_map/all_gather | solution.py:101
  8.7 124.0 %all-gather.8.cloned.1.call-start = ((), (), s32[]{:S(2)}) async-start(), calls=%async_computation.15 | async-start | bytes 2228224 | tf_op jit(solution)/shard_map/all_gather | solution.py:99
  9.5 235.5 %all-gather.14.cloned.1.call-start = ((), (), s32[]{:S(2)}) async-start(), calls=%async_computation.18 | async-start | bytes 2228224 | tf_op jit(solution)/shard_map/all_gather | solution.py:104
  10.0 246.7 %all-gather.16.cloned.1.call-start = ((), (), s32[]{:S(2)}) async-start(), calls=%async_computation.19 | async-start | bytes 10027008 | tf_op jit(solution)/shard_map/all_gather | solution.py:108
  10.6 327.6 %all-gather.18.cloned.1.call-start = ((), (), s32[]{:S(2)}) async-start(), calls=%async_computation.20 | async-start | bytes 10027008 | tf_op jit(solution)/shard_map/all_gather | solution.py:109
  11.2 408.7 %all-gather.20.cloned.1.call-start = ((), (), s32[]{:S(2)}) async-start(), calls=%async_computation.21 | async-start | bytes 10027008 | tf_op jit(solution)/shard_map/all_gather | solution.py:110
  51.7 84.6 %copy-start.61 = (f32[64]{0:T(128)}, f32[64]{0:T(128)S(1)}, u32[]{:S(2)}) copy-start(f32[64]{0:T(128)S(1)} %convert_element_type.173) | copy-start | bytes 772
  52.5 2.8 copy-start.59
  52.8 80.0 %copy-start.15 = (bf16[512,1024]{1,0:T(8,128)(2,1)}, bf16[512,1024]{1,0:T(8,128)(2,1)S(1)}, u32[]{:S(2)}) copy-start(bf16[512,1024]{1,0:T(8,128)(2,1)S(1)} %multiply_convert_fusion.3) | copy-start | bytes 3145732
  53.2 87.8 %copy-start.31 = (f32[512,32]{0,1:T(8,128)}, f32[512,32]{0,1:T(8,128)S(1)}, u32[]{:S(2)}) copy-start(f32[512,32]{0,1:T(8,128)S(1)} %get-tuple-element.306) | copy-start | bytes 196612
  53.2 87.8 %copy-start.33 = (f32[512,32]{0,1:T(8,128)}, f32[512,32]{0,1:T(8,128)S(1)}, u32[]{:S(2)}) copy-start(f32[512,32]{0,1:T(8,128)S(1)} %get-tuple-element.307) | copy-start | bytes 196612
  57.2 80.3 %all-to-all-start.1 = ((bf16[512,2,256]{0,2,1:T(8,128)(2,1)}), bf16[512,2,256]{0,2,1:T(8,128)(2,1)}, u32[]{:S(2)}, u32[]{:S(2)}) async-start(bf16[512,2,256]{0,2,1:T(8,128)(2,1)} %bitcast.10), calls=%async_computation.1 | async-start | bytes 1048576 | tf_op jit(solution)/shard_map/all_to_all | solution.py:136
  137.5 12.1 all-to-all-start.2
  149.6 18.2 %all-to-all-start = ((bf16[512,2,512]{0,2,1:T(8,128)(2,1)}), bf16[512,2,512]{0,2,1:T(8,128)(2,1)}, u32[]{:S(2)}, u32[]{:S(2)}) async-start(bf16[512,2,512]{0,2,1:T(8,128)(2,1)} %bitcast.5), calls=%async_computation | async-start | bytes 2097152 | tf_op jit(solution)/shard_map/all_to_all | solution.py:129
  218.1 6.2 copy-start.64
  220.8 16.3 %all-to-all-start.3 = ((bf16[2,2,131072]{2,1,0:T(2,128)(2,1)}), bf16[2,2,131072]{2,1,0:T(2,128)(2,1)S(1)}, u32[]{:S(2)}, u32[]{:S(2)}) async-start(bf16[2,2,131072]{2,1,0:T(2,128)(2,1)} %reshape.492), calls=%async_computation.3 | async-start | bytes 2097152 | tf_op jit(solution)/shard_map/all_to_all | solution.py:174
  224.5 232.0 %copy-start.57 = (f32[512]{0:T(512)}, f32[512]{0:T(512)S(1)}, u32[]{:S(2)}) copy-start(f32[512]{0:T(512)S(1)} %dynamic-slice_convert_fusion.1) | copy-start | bytes 6148
  239.4 5.6 copy-start.5
  249.8 88.5 %copy-start.17 = (bf16[512,1024]{1,0:T(8,128)(2,1)}, bf16[512,1024]{1,0:T(8,128)(2,1)S(1)}, u32[]{:S(2)}) copy-start(bf16[512,1024]{1,0:T(8,128)(2,1)S(1)} %multiply_convert_fusion.2) | copy-start | bytes 3145732
  438.4 9.2 copy-start.20
  438.4 9.2 copy-start.24
  447.6 8.9 copy-start.29
  460.5 17.9 %all-to-all-start.4 = ((bf16[512,2,512]{2,0,1:T(8,128)(2,1)}), bf16[512,2,512]{2,0,1:T(8,128)(2,1)S(1)}, u32[]{:S(2)}, u32[]{:S(2)}) async-start(bf16[512,2,512]{2,0,1:T(8,128)(2,1)} %bitcast.213), calls=%async_computation.4 | async-start | bytes 2097152 | tf_op jit(solution)/shard_map/all_to_all | solution.py:219
  464.1 233.9 %reduce-scatter.10.cloned.1.call-start = ((), (), s32[]{:S(2)}) async-start(), calls=%async_computation.23 | async-start | bytes 2228224 | tf_op jit(solution)/shard_map/reduce_scatter | solution.py:284
  480.7 3.6 copy-start.9
  480.7 3.6 copy-start.46
  506.8 6.3 copy-start
  506.8 6.3 copy-start.1
  506.8 13.9 slice-start
  513.1 7.7 slice-start.1
  513.1 7.7 copy-start.26
  520.7 2.7 copy-start.2
  520.8 3.7 copy-start.10
  524.4 3.6 copy-start.9
  524.4 3.6 copy-start.46
  550.5 6.5 copy-start
  550.5 6.5 copy-start.1
  550.5 14.2 slice-start
  557.0 7.7 slice-start.1
  557.0 7.7 copy-start.26
  564.7 2.7 copy-start.2
  564.7 3.7 copy-start.10
  582.0 2.5 copy-start.32
  585.7 2.8 copy-start.22
  588.5 124.0 %reduce-scatter.12.cloned.1.call-start = ((), (), s32[]{:S(2)}) async-start(), calls=%async_computation.24 | async-start | bytes 2228224 | tf_op jit(solution)/shard_map/reduce_scatter | solution.py:285
  601.1 3.4 copy-start.12
  604.4 183.6 %reduce-scatter.14.cloned.1.call-start = ((), (), s32[]{:S(2)}) async-start(), calls=%async_computation.25 | async-start | bytes 4456448 | tf_op jit(solution)/shard_map/reduce_scatter | solution.py:288
  609.0 254.7 %reduce-scatter.8.cloned.1.call-start = ((), (), s32[]{:S(2)}) async-start(), calls=%async_computation.22 | async-start | bytes 4456448 | tf_op jit(solution)/shard_map/reduce_scatter | solution.py:283
  660.1 400.6 %reduce-scatter.16.cloned.1.call-start = ((), (), s32[]{:S(2)}) async-start(), calls=%async_computation.26 | async-start | bytes 20054016 | tf_op jit(solution)/shard_map/reduce_scatter | solution.py:211
  673.0 585.0 %reduce-scatter.18.cloned.1.call-start = ((), (), s32[]{:S(2)}) async-start(), calls=%async_computation.27 | async-start | bytes 20054016 | tf_op jit(solution)/shard_map/reduce_scatter | solution.py:212
  684.5 770.5 %reduce-scatter.20.cloned.1.call-start = ((), (), s32[]{:S(2)}) async-start(), calls=%async_computation.28 | async-start | bytes 20054016 | tf_op jit(solution)/shard_map/reduce_scatter | solution.py:213
  697.7 870.4 %all-reduce.19.cloned.1.call-start = ((), (), s32[]{:S(2)}) async-start(), calls=%async_computation.29 | async-start | bytes 8650752 | tf_op jit(solution)/shard_map/psum | solution.py:290
  1456.7 10.1 copy-start.23
  1456.7 10.1 copy-start.37
  1470.7 40.8 %copy-start.56 = (f32[512]{0:T(512)S(1)}, f32[512]{0:T(512)}, u32[]{:S(2)}) copy-start(f32[512]{0:T(512)} %copy-done.55) | copy-start | bytes 6148
  1568.1 9.0 copy-start.36
  1574.7 3.5 copy-start.35
  (40 other events, 57.2 us)
Sparse Core Ops, SparseCore 0:
  10.2 40.6 all-gather.9
  53.1 36.9 all-gather.11
  92.3 40.4 all-gather.7
  134.8 40.1 all-gather.13
  177.1 79.6 all-gather.15
  258.9 79.3 all-gather.17
  340.5 79.3 all-gather.19
  588.6 59.2 reduce-scatter.9
  651.7 60.7 reduce-scatter.11
  716.2 71.7 reduce-scatter.13
  791.8 71.7 reduce-scatter.7
  867.6 193.0 reduce-scatter.15
  1064.8 193.1 reduce-scatter.17
  1261.9 193.1 reduce-scatter.19
  1458.0 110.0 all-reduce.18
where the time goes:
time: 1590 us
  waiting for transfers between devices  1080 us (68%)
  matrix products  215 us (14%)
  blocking collectives  109 us (7%)
  local copies, waits for them, and re-layouts  81.3 us (5%)
  other arithmetic  66.4 us (4%)
  starting transfers between devices  20.3 us (1%)
  between operations  18.6 us (1%)
    reduce_scatter x1, waiting for transfers between devices, body(): lax.psum_scatter(d_up_w, 'dp', scatter_dimension=0, tiled=True)  197 us
    reduce_scatter x1, waiting for transfers between devices, body(): lax.psum_scatter(d_down, 'dp', scatter_dimension=0, tiled=True)  197 us
    reduce_scatter x1, waiting for transfers between devices, body(): lax.psum_scatter(d_gate_w, 'dp', scatter_dimension=0, tiled=True)  197 us
    dot_general x28, matrix products, mat_dot(): return jnp.einsum(form, left, right, preferred_element_type=jnp.float32)  171 us
    reduce_scatter x1, waiting for transfers between devices, body(): lax.psum_scatter(d_query_w, 'dp', scatter_dimension=0, tiled=True)  75.7 us
    reduce_scatter x1, waiting for transfers between devices, body(): lax.psum_scatter(d_out_w, 'dp', scatter_dimension=0, tiled=True)  75.5 us
    all_gather x1, waiting for transfers between devices, body(): lax.all_gather(w_down, 'dp', axis=0, tiled=True)  70.5 us
    all_gather x1, waiting for transfers between devices, body(): lax.all_gather(w_up, 'dp', axis=0, tiled=True)  70.4 us
  transfers between devices with their start and end apart: 20, of which 16 were waited for; matrix products, arithmetic and copies ran while one was open for 13% of the time, Pallas kernels for 0%

commit v1 on v0

v1 whole, which is shorter than its diff:
```python
from functools import partial
import math

import jax
import jax.numpy as jnp
from jax import lax
from jax.experimental import pallas as pl
from jax.experimental.pallas import tpu as pltpu
from jax.sharding import PartitionSpec as P

H = 16
KV = 8
HD = 64
GROUP = H // KV
MINLEN = 1024

EPSILON = 1e-05
ROPE_BASE = 1000000.0
MASKED_SCORE = -1e30
BF = jnp.bfloat16
F32 = jnp.float32


def dot(left, right, lc, rc):
    return lax.dot_general(left, right, (((lc,), (rc,)), ((), ())), preferred_element_type=F32)


def masked(scores, q0, k0, segs):
    row = lax.broadcasted_iota(jnp.int32, scores.shape, 0) + k0
    col = lax.broadcasted_iota(jnp.int32, scores.shape, 1) + q0
    allowed = row <= col
    if segs is not None:
        allowed = allowed & (segs[0] == segs[1])
    return jnp.where(allowed, scores, MASKED_SCORE)


def attn_fwd_kernel(blk, static, *refs):
    if static:
        q_ref, k_ref, v_ref, o_ref, lse_ref = refs
    else:
        q_ref, k_ref, v_ref, sc_ref, sr_ref, o_ref, lse_ref = refs
    length = q_ref.shape[1]
    keys = k_ref[...].T

    def finish(q0, parts):
        top = parts[0][0].max(axis=0, keepdims=True)
        for s, _ in parts[1:]:
            top = jnp.maximum(top, s.max(axis=0, keepdims=True))
        total, out = 0.0, 0.0
        for s, v in parts:
            p = jnp.exp(s - top)
            total = total + p.sum(axis=0, keepdims=True)
            out = out + dot(v, p.astype(BF), 1, 0)
        o_ref[:, pl.ds(q0, blk)] = (out / total).astype(BF)
        lse_ref[0, :, pl.ds(q0, blk)] = top + jnp.log(total)

    if static:
        for qb in range(length // blk):
            q0 = qb * blk
            q = q_ref[:, q0 : q0 + blk]
            parts = []
            if qb:
                parts.append((dot(keys[:q0], q, 1, 0), v_ref[:, :q0]))
            diag = masked(dot(keys[q0 : q0 + blk], q, 1, 0), 0, 0, None)
            parts.append((diag, v_ref[:, q0 : q0 + blk]))
            finish(q0, parts)
    else:

        @pl.loop(0, length // blk)
        def _(qb):
            q0 = pl.multiple_of(qb * blk, blk)
            s = dot(keys, q_ref[:, pl.ds(q0, blk)], 1, 0)
            s = masked(s, q0, 0, (sc_ref[...], sr_ref[:, pl.ds(q0, blk)]))
            finish(q0, [(s, v_ref[...])])


def attn_bwd_kernel(blk, static, *refs):
    if static:
        q_ref, k_ref, v_ref, do_ref, o_ref, lse_ref, dq_ref, dk_ref, dv_ref, dk_acc, dv_acc = refs
    else:
        (q_ref, k_ref, v_ref, do_ref, o_ref, lse_ref, sc_ref, sr_ref,
         dq_ref, dk_ref, dv_ref, dk_acc, dv_acc) = refs
    length = q_ref.shape[1]
    member = lax.rem(pl.program_id(0), GROUP)
    keys = k_ref[...].T
    values = v_ref[...].T

    @pl.when(member == 0)
    def _():
        dk_acc[...] = jnp.zeros_like(dk_acc)
        dv_acc[...] = jnp.zeros_like(dv_acc)

    def part(q, d_out, lse, delta, k_lo, k_n, q0, segs, mask):
        rows = pl.ds(k_lo, k_n)
        k_blk, v_blk = keys[k_lo : k_lo + k_n], values[k_lo : k_lo + k_n]
        s = dot(k_blk, q, 1, 0)
        if mask:
            s = masked(s, q0, k_lo, segs)
        p = jnp.exp(s - lse)
        dv_acc[rows, :] += dot(p.astype(BF), d_out, 1, 1)
        dp = dot(v_blk, d_out, 1, 0)
        ds = (p * (dp - delta)).astype(BF)
        dk_acc[rows, :] += dot(ds, q, 1, 1)
        return dot(k_ref[:, rows], ds, 1, 0)

    def prepare(q0):
        cols = pl.ds(q0, blk)
        d_out = do_ref[:, cols]
        delta = (d_out.astype(F32) * o_ref[:, cols].astype(F32)).sum(axis=0, keepdims=True)
        return cols, q_ref[:, cols], d_out, lse_ref[0, :, cols], delta

    scale = 1.0 / math.sqrt(HD)
    if static:
        for qb in range(length // blk):
            q0 = qb * blk
            cols, q, d_out, lse, delta = prepare(q0)
            dq = part(q, d_out, lse, delta, q0, blk, q0, None, True)
            if qb:
                dq = dq + part(q, d_out, lse, delta, 0, q0, q0, None, False)
            dq_ref[:, cols] = (dq * scale).astype(BF)
    else:

        @pl.loop(0, length // blk)
        def _(qb):
            q0 = pl.multiple_of(qb * blk, blk)
            cols, q, d_out, lse, delta = prepare(q0)
            dq = part(q, d_out, lse, delta, 0, length, q0, (sc_ref[...], sr_ref[:, cols]), True)
            dq_ref[:, cols] = (dq * scale).astype(BF)

    @pl.when(member == GROUP - 1)
    def _():
        dk_ref[...] = dk_acc[...].T.astype(BF)
        dv_ref[...] = dv_acc[...].T.astype(BF)


def attn_specs(length):
    q_spec = pl.BlockSpec((HD, length), lambda h: (h, 0))
    kv_spec = pl.BlockSpec((HD, length), lambda h: (h // GROUP, 0))
    lse_spec = pl.BlockSpec((1, 1, length), lambda h: (h, 0, 0))
    seg_specs = [
        pl.BlockSpec((length, 1), lambda h: (0, 0)),
        pl.BlockSpec((1, length), lambda h: (0, 0)),
    ]
    return q_spec, kv_spec, lse_spec, seg_specs


def attn_fwd(q, k, v, segs):
    rows, length = q.shape
    heads = rows // HD
    static = segs is None
    q_spec, kv_spec, lse_spec, seg_specs = attn_specs(length)
    extra = () if static else (segs[:, None], segs[None, :])
    return pl.pallas_call(
        partial(attn_fwd_kernel, min(256, length), static),
        grid=(heads,),
        in_specs=[q_spec, kv_spec, kv_spec] + ([] if static else seg_specs),
        out_specs=[q_spec, lse_spec],
        out_shape=[
            jax.ShapeDtypeStruct((rows, length), BF),
            jax.ShapeDtypeStruct((heads, 1, length), F32),
        ],
        cost_estimate=pl.CostEstimate(
            flops=4 * heads * length * length * HD,
            transcendentals=heads * length * length,
            bytes_accessed=4 * rows * length * 2,
        ),
        name="attn_fwd",
    )(q, k, v, *extra)


def attn_bwd(q, k, v, d_out, out, lse, segs):
    rows, length = q.shape
    heads = rows // HD
    static = segs is None
    q_spec, kv_spec, lse_spec, seg_specs = attn_specs(length)
    extra = () if static else (segs[:, None], segs[None, :])
    return pl.pallas_call(
        partial(attn_bwd_kernel, min(256, length), static),
        grid=(heads,),
        in_specs=[q_spec, kv_spec, kv_spec, q_spec, q_spec, lse_spec]
        + ([] if static else seg_specs),
        out_specs=[q_spec, kv_spec, kv_spec],
        out_shape=[
            jax.ShapeDtypeStruct((rows, length), BF),
            jax.ShapeDtypeStruct(k.shape, BF),
            jax.ShapeDtypeStruct(v.shape, BF),
        ],
        scratch_shapes=[pltpu.VMEM((length, HD), F32), pltpu.VMEM((length, HD), F32)],
        cost_estimate=pl.CostEstimate(
            flops=10 * heads * length * length * HD,
            transcendentals=heads * length * length,
            bytes_accessed=7 * rows * length * 2,
        ),
        name="attn_bwd",
    )(q, k, v, d_out, out, lse, *extra)


def pick(arr, index, axis):
    return lax.dynamic_index_in_dim(arr, index, axis, keepdims=False)


def ordered(mine, other, rank, axis):
    low_ = jnp.where(rank == 0, mine, other)
    high = jnp.where(rank == 0, other, mine)
    return jnp.stack([low_, high], axis=axis)


def dp_gather(shard):
    count = lax.axis_size("dp")
    if count != 16:
        return lax.all_gather(shard, "dp", axis=0, tiled=False)
    index = lax.axis_index("dp")
    z, x, core = index // 4, (index // 2) % 2, index % 2
    got = [shard] + [
        lax.ppermute(shard, "dp", [(j, (j - 4 * s) % 16) for j in range(16)]) for s in (1, 2, 3)
    ]
    ring = jnp.stack(got + got[:3])
    column = lax.dynamic_slice_in_dim(ring, (4 - z) % 4, 4, 0)
    over_x = lax.ppermute(column, "dp", [(j, j ^ 2) for j in range(16)])
    plane = ordered(column, over_x, x, 1)
    over_core = lax.ppermute(plane, "dp", [(j, j ^ 1) for j in range(16)])
    return ordered(plane, over_core, core, 2).reshape((16,) + shard.shape)


def dp_scatter(parts):
    count = lax.axis_size("dp")
    if count != 16:
        flat = parts.reshape((-1,) + parts.shape[2:])
        return lax.psum_scatter(flat, "dp", scatter_dimension=0, tiled=True).astype(F32)
    index = lax.axis_index("dp")
    z, x, core = index // 4, (index // 2) % 2, index % 2
    cube = parts.reshape((4, 2, 2) + parts.shape[1:])
    got = lax.ppermute(pick(cube, 1 - core, 2), "dp", [(j, j ^ 1) for j in range(16)])
    square = (pick(cube, core, 2).astype(F32) + got.astype(F32)).astype(BF)
    got = lax.ppermute(pick(square, 1 - x, 1), "dp", [(j, j ^ 2) for j in range(16)])
    line = (pick(square, x, 1).astype(F32) + got.astype(F32)).astype(BF)
    total = pick(line, z, 0).astype(F32)
    for s in (1, 2, 3):
        got = lax.ppermute(
            pick(line, (z + s) % 4, 0), "dp", [(j, (j + 4 * s) % 16) for j in range(16)]
        )
        total = total + got.astype(F32)
    return total


def seq_swap(arr):
    return lax.ppermute(arr, "seq", [(0, 1), (1, 0)])


def seq_tokens(rows):
    if lax.axis_size("seq") == 2:
        return jnp.concatenate([rows, seq_swap(rows)], axis=0)
    return lax.all_gather(rows, "seq", axis=0, tiled=True)


def seq_tokens_sum(parts):
    if lax.axis_size("seq") == 2:
        own = parts.shape[0] // 2
        return parts[:own] + seq_swap(parts[own:].astype(BF)).astype(F32)
    return lax.psum_scatter(parts.astype(BF), "seq", scatter_dimension=0, tiled=True).astype(F32)


def seq_stack(arr):
    if lax.axis_size("seq") == 2:
        return ordered(arr, seq_swap(arr), lax.axis_index("seq"), 0)
    return lax.all_gather(arr, "seq", axis=0, tiled=False)


def heads_to_tokens(arr):
    count = lax.axis_size("seq")
    rows, length = arr.shape
    if count == 2:
        rank = lax.axis_index("seq")
        own = length // 2
        mine = lax.dynamic_slice_in_dim(arr, rank * own, own, 1)
        theirs = seq_swap(lax.dynamic_slice_in_dim(arr, (1 - rank) * own, own, 1))
        return ordered(mine, theirs, rank, 0).reshape(2 * rows, own)
    return lax.all_to_all(arr, "seq", split_axis=1, concat_axis=0, tiled=True)


def tokens_to_heads(arr):
    count = lax.axis_size("seq")
    rows, own = arr.shape
    if count == 2:
        rank = lax.axis_index("seq")
        half = rows // 2
        mine = lax.dynamic_slice_in_dim(arr, rank * half, half, 0)
        theirs = seq_swap(lax.dynamic_slice_in_dim(arr, (1 - rank) * half, half, 0))
        first = jnp.where(rank == 0, mine, theirs)
        second = jnp.where(rank == 0, theirs, mine)
        return jnp.concatenate([first, second], axis=1)
    return lax.all_to_all(arr, "seq", split_axis=0, concat_axis=1, tiled=True)


def pack_layout(seq_lens, total):
    places = jnp.arange(total, dtype=jnp.int32)
    ends = jnp.cumsum(seq_lens)
    starts = ends - seq_lens
    segment = jnp.sum((places[:, None] >= ends[None, :]).astype(jnp.int32), axis=1)
    starts_ext = jnp.concatenate([starts, ends[-1:]])
    labels = jnp.arange(seq_lens.shape[0] + 1, dtype=jnp.int32)
    offset = jnp.sum(jnp.where(segment[:, None] == labels[None, :], starts_ext[None, :], 0), axis=1)
    return segment, places - offset, segment < seq_lens.shape[0]


def unit_rms(values):
    inv = lax.rsqrt(jnp.mean(values * values, axis=-1, keepdims=True) + EPSILON)
    return values * inv, inv


def unit_rms_back(y, xhat, inv):
    return inv * (y - xhat * jnp.mean(y * xhat, axis=-1, keepdims=True))


def head_prep(lin, gain, cos_tab, sin_tab, scale):
    u = lin.reshape(-1, HD, lin.shape[1])
    inv = lax.rsqrt(jnp.mean(u * u, axis=1, keepdims=True) + EPSILON)
    u = u * inv * gain[None, :, None]
    first, second = u[:, : HD // 2], u[:, HD // 2 :]
    out = jnp.concatenate(
        [first * cos_tab - second * sin_tab, second * cos_tab + first * sin_tab], axis=1
    )
    return (out * scale).astype(BF).reshape(lin.shape)


def head_prep_back(grad, lin, gain, cos_tab, sin_tab):
    y = grad.astype(F32).reshape(-1, HD, lin.shape[1])
    first, second = y[:, : HD // 2], y[:, HD // 2 :]
    y = jnp.concatenate(
        [first * cos_tab + second * sin_tab, second * cos_tab - first * sin_tab], axis=1
    )
    u = lin.reshape(y.shape)
    inv = lax.rsqrt(jnp.mean(u * u, axis=1, keepdims=True) + EPSILON)
    xhat = u * inv
    d_gain = jnp.sum(y * xhat, axis=(0, 2))
    y = y * gain[None, :, None]
    d_lin = inv * (y - xhat * jnp.mean(y * xhat, axis=1, keepdims=True))
    return d_lin.astype(BF).reshape(lin.shape), d_gain


def body(
    tokens, lengths, attn_gain, w_query, w_key, w_value, query_gain, key_gain, w_out,
    ffn_gain, w_gate, w_up, w_down, cotangent,
):
    seq_n = lax.axis_size("seq")
    dp_n = lax.axis_size("dp")
    rank = lax.axis_index("seq")
    dp_rank = lax.axis_index("dp")
    own, width = tokens.shape
    length = own * seq_n
    q_w, kv_w = H * HD // seq_n, KV * HD // seq_n
    ff_dp = w_down.shape[0]
    ff_w = ff_dp // seq_n
    ff = ff_w * dp_n
    d_dp = w_query.shape[0]

    full = length == MINLEN * lengths.shape[1]
    segment, positions, valid = pack_layout(lengths[0], length)
    segs = None if full and lengths.shape[1] == 1 else segment
    my_valid = lax.dynamic_slice_in_dim(valid, rank * own, own).astype(F32)[:, None]

    def keep_valid(arr):
        return arr if full else arr * my_valid

    gain_a = attn_gain.astype(F32)[:, None]
    gain_f = ffn_gain.astype(F32)[:, None]

    def my_cols(w, n):
        return lax.dynamic_slice_in_dim(w, rank * n, n, 1)

    qkv_part = jnp.concatenate(
        [my_cols(w_query, q_w), my_cols(w_key, kv_w), my_cols(w_value, kv_w)], axis=1
    )
    qkv_part = (qkv_part.astype(F32) * gain_a).astype(BF)
    gains = jnp.concatenate([query_gain, key_gain])
    gains = jnp.pad(gains[None, :], ((0, 7), (0, qkv_part.shape[1] - gains.shape[0])))
    pick_ff = lambda w: pick(w.reshape(d_dp, dp_n, seq_n, ff_w), rank, 2).reshape(d_dp, ff)
    gu_part = jnp.concatenate([pick_ff(w_gate), pick_ff(w_up)], axis=1)
    gu_part = (gu_part.astype(F32) * gain_f).astype(BF)
    down_part = pick(w_down.reshape(seq_n, ff_w, width), rank, 0)

    gu_full = lax.all_gather(gu_part, "dp", axis=0, tiled=True)
    down_full = lax.all_gather(down_part, "dp", axis=0, tiled=True)
    got = dp_gather(jnp.concatenate([qkv_part, gains], axis=0))
    qkv_full = got[:, :d_dp].reshape(width, -1)
    per = query_gain.shape[0]
    gain_q = got[:, d_dp, :per].reshape(-1).astype(F32)
    gain_k = got[:, d_dp, per : 2 * per].reshape(-1).astype(F32)
    out_full = dp_gather(w_out).reshape(H * HD, width)

    xhat_a, inv_a = unit_rms(tokens)
    low_own = xhat_a.astype(BF)
    if seq_n == 2:
        low_a = ordered(low_own, seq_swap(low_own), rank, 0).reshape(length, width)
    else:
        low_a = lax.all_gather(low_own, "seq", axis=0, tiled=True)
    lin = dot(qkv_full, low_a, 0, 1)
    q_lin, k_lin = lin[:q_w], lin[q_w : q_w + kv_w]
    values = lin[q_w + kv_w :].astype(BF)
    freqs = ROPE_BASE ** (-(jnp.arange(HD // 2, dtype=F32) * (2.0 / HD)))
    angles = freqs[:, None] * positions.astype(F32)[None, :]
    cos_tab, sin_tab = jnp.cos(angles), jnp.sin(angles)
    queries = head_prep(q_lin, gain_q, cos_tab, sin_tab, 1.0 / math.sqrt(HD))
    keys = head_prep(k_lin, gain_k, cos_tab, sin_tab, 1.0)
    att_heads, lse = attn_fwd(queries, keys, values, segs)
    attended = heads_to_tokens(att_heads)
    resid = tokens + dot(attended, out_full, 0, 0)

    xhat_f, inv_f = unit_rms(resid)
    grad = keep_valid(cotangent)
    x_all = seq_tokens(xhat_f.astype(BF))
    g_all = seq_tokens(grad.astype(BF))
    gate = dot(x_all, gu_full[:, :ff], 1, 0)
    up = dot(x_all, gu_full[:, ff:], 1, 0)
    d_hidden = dot(g_all, down_full, 1, 1)
    sig = jax.nn.sigmoid(gate)
    silu = gate * sig
    hidden = (silu * up).astype(BF)
    d_gate = (d_hidden * up * sig * (1.0 + gate * (1.0 - sig))).astype(BF)
    d_up = (d_hidden * silu).astype(BF)
    d_ffn = dot(d_gate, gu_full[:, :ff], 1, 1) + dot(d_up, gu_full[:, ff:], 1, 1)
    d_ffn = seq_tokens_sum(d_ffn)
    d_resid = grad + unit_rms_back(d_ffn, xhat_f, inv_f)

    block_out = keep_valid(resid + seq_tokens_sum(dot(hidden, down_full, 1, 0)))
    d_w_g = dp_scatter(dot(x_all, d_gate, 0, 0).astype(BF).reshape(dp_n, d_dp, ff))
    d_w_u = dp_scatter(dot(x_all, d_up, 0, 0).astype(BF).reshape(dp_n, d_dp, ff))
    d_w_d = dp_scatter(dot(hidden, g_all, 0, 0).astype(BF).reshape(dp_n, ff_w, width))

    def full_ff(shard):
        both = seq_stack(shard.astype(BF)).reshape(seq_n, d_dp, dp_n, ff_w)
        return both.transpose(1, 2, 0, 3).reshape(d_dp, dp_n * seq_n * ff_w).astype(F32)

    d_w_g, d_w_u = full_ff(d_w_g), full_ff(d_w_u)
    d_w_d = seq_stack(d_w_d.astype(BF)).reshape(ff_dp, width).astype(F32)
    d_ffn_gain = jnp.sum(w_gate.astype(F32) * d_w_g + w_up.astype(F32) * d_w_u, axis=1)

    r_low = d_resid.astype(BF)
    d_att = tokens_to_heads(dot(out_full, r_low, 1, 1).astype(BF))
    d_w_o = dp_scatter(dot(attended, r_low, 1, 0).astype(BF).reshape(dp_n, d_dp, width))
    d_q, d_k, d_v = attn_bwd(queries, keys, values, d_att, att_heads, lse, segs)
    d_q, d_gq = head_prep_back(d_q, q_lin, gain_q, cos_tab, sin_tab)
    d_k, d_gk = head_prep_back(d_k, k_lin, gain_k, cos_tab, sin_tab)
    d_lin = jnp.concatenate([d_q, d_k, d_v], axis=0)
    d_norm = dot(d_lin, qkv_full, 0, 1)
    if seq_n == 2:
        other = lax.dynamic_slice_in_dim(d_norm, (1 - rank) * own, own, 0)
        d_norm = lax.dynamic_slice_in_dim(d_norm, rank * own, own, 0)
        d_norm = d_norm + seq_swap(other.astype(BF)).astype(F32)
    else:
        d_norm = seq_tokens_sum(d_norm)
    d_tokens = d_resid + unit_rms_back(d_norm, xhat_a, inv_a)

    d_w_x = dot(low_a, d_lin, 0, 1).astype(BF).reshape(dp_n, d_dp, -1)
    d_g = jnp.concatenate([d_gq, d_gk]).astype(BF)
    d_g = jnp.pad(d_g[None, :], ((0, 7), (0, d_w_x.shape[2] - d_g.shape[0])))
    d_g = jnp.broadcast_to(d_g[None], (dp_n,) + d_g.shape)
    d_w_x = dp_scatter(jnp.concatenate([d_w_x, d_g], axis=1))
    d_w_x = seq_stack(d_w_x.astype(BF)).astype(F32)
    both = d_w_x[:, :d_dp]
    join = lambda lo, n: both[:, :, lo : lo + n].transpose(1, 0, 2).reshape(d_dp, seq_n * n)
    d_w_q, d_w_k, d_w_v = join(0, q_w), join(q_w, kv_w), join(q_w + kv_w, kv_w)
    d_gains = jnp.sum(d_w_x[:, d_dp, : 2 * HD], axis=0)
    d_gq = lax.dynamic_slice_in_dim(d_gains, dp_rank * per, per)
    d_gk = lax.dynamic_slice_in_dim(d_gains, HD + dp_rank * per, per)
    d_attn_gain = jnp.sum(w_query.astype(F32) * d_w_q, axis=1) + jnp.sum(
        w_key.astype(F32) * d_w_k + w_value.astype(F32) * d_w_v, axis=1
    )
    d_w_o = jnp.sum(seq_stack(d_w_o.astype(BF)).astype(F32), axis=0)
    return (
        block_out,
        d_tokens,
        d_attn_gain,
        d_w_q * gain_a,
        d_w_k * gain_a,
        d_w_v * gain_a,
        d_gq,
        d_gk,
        d_w_o,
        d_ffn_gain,
        d_w_g * gain_f,
        d_w_u * gain_f,
        d_w_d,
    )


def solution(mesh):
    rows, shard, vec = P(("dp", "seq"), None), P("dp", None), P("dp")
    return jax.shard_map(
        body,
        mesh=mesh,
        in_specs=(
            rows, shard, vec, shard, shard, shard, vec, vec, shard, vec, shard, shard, shard, rows,
        ),
        out_specs=(
            rows, rows, vec, shard, shard, shard, vec, vec, shard, vec, shard, shard, shard,
        ),
        check_vma=False,
    )
```

time: 1590 us -> 572 us (0.36)
  waiting for transfers between devices: 1080 us -> 229 us
  matrix products: 215 us -> 95.8 us
  blocking collectives: 109 us -> 0 us
  Pallas kernels: 0 us -> 37.5 us
  starting transfers between devices: 20.3 us -> 57.6 us
  local copies, waits for them, and re-layouts: 81.3 us -> 63 us
    reduce_scatter x7 -> x0, waiting for transfers between devices: 757 us -> none  [the longest x1 197 us: body(): lax.psum_scatter(d_up_w, 'dp', scatter_dimension=0, tiled=True)]
    ppermute x0 -> x48, waiting for transfers between devices: none -> 229 us  [the longest x13 78.3 us: seq_swap(): return lax.ppermute(arr, 'seq', [(0, 1), (1, 0)])]
    all_gather x7 -> x2, waiting for transfers between devices: 216 us -> 0.01 us  [the longest x1 0.01 us: body(): down_full = lax.all_gather(down_part, 'dp', axis=0, tiled=True)]
    dot_general x35 -> x15, matrix products: 215 us -> 95.8 us  [dot(): lax.dot_general(left, right, (((lc,), (rc,)), ((), ())), preferred_elemen...]
    unnamed x2 -> x0, blocking collectives: 68.6 us -> none
    ppermute x0 -> x48, starting transfers between devices: none -> 57.5 us  [the longest x15 19.2 us: dp_scatter(): lax.ppermute(pick(line, (z + s) % 4, 0), 'dp', [(j, (j + 4 * s) % 16) for...]
    psum x1 -> x0, waiting for transfers between devices: 52.5 us -> none  [body(): lax.psum((attn_shards[0], attn_shards[1], attn_shards[2], attn_shards[3],...]
    all_to_all x5 -> x0, waiting for transfers between devices: 44.7 us -> none  [the longest x1 14.2 us: body(): lax.all_to_all(d_attended.reshape(tok_rows, seq_count, -1), 'seq', split_...]
  transfers between devices with their start and end apart: 20 -> 50, of which waited for: 16 -> 22; matrix products, arithmetic and copies ran while one was open for 13% -> 28% of each run, Pallas kernels for 0% -> 7%
where the time goes in v1:
time: 572 us; the launch traced here: 565 us
  waiting for transfers between devices  229 us (40%)
  matrix products  95.8 us (17%)
  other arithmetic  66 us (12%)
  local copies, waits for them, and re-layouts  63 us (11%)
  starting transfers between devices  57.6 us (10%)
  Pallas kernels  37.5 us (7%)
  between operations  16.5 us (3%)
    dot_general x15, matrix products, dot(): lax.dot_general(left, right, (((lc,), (rc,)), ((), ())), preferred_elemen...  95.8 us
    ppermute x13, waiting for transfers between devices, seq_swap(): return lax.ppermute(arr, 'seq', [(0, 1), (1, 0)])  78.3 us
    ppermute x5, waiting for transfers between devices, dp_scatter(): lax.ppermute(pick(square, 1 - x, 1), 'dp', [(j, j ^ 2) for j in range(16)])  58.9 us
    ppermute x15, waiting for transfers between devices, dp_scatter(): lax.ppermute(pick(line, (z + s) % 4, 0), 'dp', [(j, (j + 4 * s) % 16) for...  36.9 us
    ppermute x6, waiting for transfers between devices, dp_gather(): lax.ppermute(shard, 'dp', [(j, (j - 4 * s) % 16) for j in range(16)])  29.6 us
    ppermute x2, waiting for transfers between devices, dp_gather(): over_x = lax.ppermute(column, 'dp', [(j, j ^ 2) for j in range(16)])  24.8 us
    pallas_call x1, Pallas kernels, attn_bwd(): pl.pallas_call(partial(attn_bwd_kernel, min(256, length), static), grid=(...  22.4 us
    ppermute x15, starting transfers between devices, dp_scatter(): lax.ppermute(pick(line, (z + s) % 4, 0), 'dp', [(j, (j + 4 * s) % 16) for...  19.2 us
  transfers between devices with their start and end apart: 50, of which 22 were waited for; matrix products, arithmetic and copies ran while one was open for 28% of the time, Pallas kernels for 7%

profile of v1, /device:TPU:0, one launch (start us, length us, event | category | flops | bytes accessed | tf_op | source)
XLA Modules:
  0.0 564.9 jit_solution(8107856118719895792)
XLA Ops:
  9.1 4.7 reshape.355
  13.8 1.8 reshape.357
  15.6 6.7 %dynamic-slice_reduce_fusion = (bf16[64,16,144]{2,1,0:T(8,128)(2,1)S(1)}, bf16[64,16,144]{2,1,0:T(8,128)(2,1)S(1)}) fusion(bf16[64,16,2,144]{3,2,1,0:T(2,128)(2,1)S(1)} %reshape.357, s32[]{:T(128)S(6)} %select_n.364, bf16[64,16,2,144]{3,2,1,0:T(2,128)(2,1)S(1)} %reshape.355), kind=kLoop, calls=%fused_computation.119 | loop fusion | bytes 1179652 | tf_op jit(solution)/shard_map/jit(dynamic_index_in_dim)/dynamic_slice | solution.py:199
  24.6 5.1 collective-permute-start.7
  32.0 2.8 collective-permute-start
  41.2 5.5 collective-permute-done.8
  50.0 24.1 %collective-permute-done.1 = bf16[72,1024]{1,0:T(8,128)(2,1)S(1)} collective-permute-done((bf16[72,1024]{1,0:T(8,128)(2,1)}, bf16[72,1024]{1,0:T(8,128)(2,1)S(1)}, u32[]{:S(2)}, u32[]{:S(2)}) %collective-permute-start.1) | collective-permute-done | bytes 147488 | tf_op jit(solution)/shard_map/ppermute | solution.py:215
  80.1 10.4 %collective-permute-done.3 = bf16[4,72,1024]{2,1,0:T(8,128)(2,1)S(1)} collective-permute-done((bf16[4,72,1024]{2,1,0:T(8,128)(2,1)S(1)}, bf16[4,72,1024]{2,1,0:T(8,128)(2,1)S(1)}, u32[]{:S(2)}, u32[]{:S(2)}) %collective-permute-start.3) | collective-permute-done | bytes 589856 | tf_op jit(solution)/shard_map/ppermute | solution.py:219
  92.3 14.4 %collective-permute-done.10 = bf16[4,64,1024]{2,1,0:T(8,128)(2,1)} collective-permute-done((bf16[4,64,1024]{2,1,0:T(8,128)(2,1)}, bf16[4,64,1024]{2,1,0:T(8,128)(2,1)}, u32[]{:S(2)}, u32[]{:S(2)}) %collective-permute-start.10) | collective-permute-done | bytes 524320 | tf_op jit(solution)/shard_map/ppermute | solution.py:219
  116.3 4.6 fusion.73
  126.3 15.1 %attn_fwd.1 = (bf16[512,1024]{1,0:T(8,128)(2,1)}, f32[8,1,1024]{2,1,0:T(1,128)}) custom-call(bf16[512,1024]{1,0:T(8,128)(2,1)} %bitcast.307, bf16[256,1024]{1,0:T(8,128)(2,1)} %bitcast.316, bf16[256,1024]{1,0:T(8,128)(2,1)} %slice.182.refs_2_), custom_call_target="tpu_custom_call" | custom-call | flops 2147483648 | bytes 4194304 | tf_op jit(solution)/shard_map/attn_fwd/pallas_call | solution.py:153
  148.1 9.3 %collective-permute-done.6 = bf16[512,512]{1,0:T(8,128)(2,1)S(1)} collective-permute-done((bf16[512,512]{1,0:T(8,128)(2,1)S(1)}, bf16[512,512]{1,0:T(8,128)(2,1)S(1)}, u32[]{:S(2)}, u32[]{:S(2)}) %collective-permute-start.6) | collective-permute-done | bytes 524320 | tf_op jit(solution)/shard_map/ppermute | solution.py:247
  163.3 16.7 %collective-permute-done.14 = bf16[512,1024]{1,0:T(8,128)(2,1)} collective-permute-done((bf16[512,1024]{1,0:T(8,128)(2,1)S(1)}, bf16[512,1024]{1,0:T(8,128)(2,1)}, u32[]{:S(2)}, u32[]{:S(2)}) %collective-permute-start.14) | collective-permute-done | bytes 1048608 | tf_op jit(solution)/shard_map/ppermute | solution.py:247
  180.0 10.1 %fusion.4 = f32[1024,2304]{1,0:T(8,128)} fusion(bf16[1,2304,1024]{2,1,0:T(8,128)(2,1)} %all-gather.6.cloned.1.call-done, bf16[512,1024]{1,0:T(8,128)(2,1)} %collective-permute-done.14, bf16[512,1024]{1,0:T(8,128)(2,1)S(1)} %convert_element_type.416), kind=kOutput, calls=%fused_computation.14 | convolution fusion | flops 4836032512 | bytes 16252928 | tf_op jit(solution)/shard_map/dot_general | solution.py:25
  190.1 11.8 %collective-permute-done.12 = bf16[512,1024]{1,0:T(8,128)(2,1)} collective-permute-done((bf16[512,1024]{1,0:T(8,128)(2,1)}, bf16[512,1024]{1,0:T(8,128)(2,1)}, u32[]{:S(2)}, u32[]{:S(2)}) %collective-permute-start.12) | collective-permute-done | bytes 1048608 | tf_op jit(solution)/shard_map/ppermute | solution.py:247
  202.0 11.6 %fusion.10 = f32[1024,2304]{1,0:T(8,128)} fusion(bf16[1024,4608]{1,0:T(8,128)(2,1)} %all-gather.4.cloned.1.call-done, bf16[512,1024]{1,0:T(8,128)(2,1)} %collective-permute-done.12, bf16[512,1024]{1,0:T(8,128)(2,1)} %multiply_convert_fusion.3), kind=kOutput, calls=%fused_computation.20 | convolution fusion | flops 4836032512 | bytes 16252928 | tf_op jit(solution)/shard_map/dot_general | solution.py:25
  213.6 16.9 %multiply_convert_fusion.1 = (bf16[1024,2304]{1,0:T(8,128)(2,1)}, bf16[1024,2304]{1,0:T(8,128)(2,1)}, bf16[1024,2304]{1,0:T(8,128)(2,1)}) fusion(f32[1024,2304]{1,0:T(8,128)} %fusion.4, f32[1024,2304]{1,0:T(8,128)} %fusion.10, bf16[1024,4608]{1,0:T(8,128)(2,1)} %all-gather.4.cloned.1.call-done, bf16[512,1024]{1,0:T(8,128)(2,1)} %collective-permute-done.12, ...), kind=kOutput, calls=%fused_computation.1 | convolution fusion | flops 4871421952 | bytes 39845888 | tf_op jit(solution)/shard_map/dot_general | solution.py:25
  230.5 8.0 %convolution_convert_fusion = bf16[2304,1024]{1,0:T(8,128)(2,1)S(1)} fusion(bf16[1024,2304]{1,0:T(8,128)(2,1)} %get-tuple-element.27, bf16[512,1024]{1,0:T(8,128)(2,1)} %collective-permute-done.14, bf16[512,1024]{1,0:T(8,128)(2,1)S(1)} %convert_element_type.416), kind=kOutput, calls=%fused_computation.5 | convolution fusion | flops 4838391808 | bytes 11534336 | tf_op jit(solution)/shard_map/dot_general | solution.py:25
  240.3 1.8 copy-done.13
  242.1 8.3 %convolution_convert_fusion.2 = bf16[1024,2304]{1,0:T(8,128)(2,1)S(1)} fusion(bf16[1024,2304]{1,0:T(8,128)(2,1)S(1)} %copy-done.50, bf16[512,1024]{1,0:T(8,128)(2,1)} %collective-permute-done.12, bf16[512,1024]{1,0:T(8,128)(2,1)} %multiply_convert_fusion.3), kind=kOutput, calls=%fused_computation.7 | convolution fusion | flops 4838391808 | bytes 11534336 | tf_op jit(solution)/shard_map/dot_general | solution.py:25
  250.4 1.8 dynamic-slice_bitcast_fusion.1
  253.5 5.1 fusion.8
  258.5 5.1 fusion.26
  265.3 6.9 %fusion.6 = f32[1024,1024]{1,0:T(8,128)S(1)} fusion(bf16[1024,2304]{1,0:T(8,128)(2,1)} %get-tuple-element.27, bf16[1,2304,1024]{2,1,0:T(8,128)(2,1)S(1)} %bitcast.323), kind=kOutput, calls=%fused_computation.16 | convolution fusion | flops 4831838208 | bytes 13631488 | tf_op jit(solution)/shard_map/dot_general | solution.py:25
  273.4 7.7 %convolution_convert_fusion.1 = bf16[1024,2304]{1,0:T(8,128)(2,1)S(1)} fusion(bf16[1024,2304]{1,0:T(8,128)(2,1)S(1)} %bitcast.327, bf16[512,1024]{1,0:T(8,128)(2,1)} %collective-permute-done.12, bf16[512,1024]{1,0:T(8,128)(2,1)} %multiply_convert_fusion.3), kind=kOutput, calls=%fused_computation.6 | convolution fusion | flops 4838391808 | bytes 11534336 | tf_op jit(solution)/shard_map/dot_general | solution.py:25
  281.1 8.8 %collective-permute-done.15 = bf16[512,1024]{1,0:T(8,128)(2,1)S(1)} collective-permute-done((bf16[512,1024]{1,0:T(8,128)(2,1)S(1)}, bf16[512,1024]{1,0:T(8,128)(2,1)S(1)}, u32[]{:S(2)}, u32[]{:S(2)}) %collective-permute-start.15) | collective-permute-done | bytes 1048608 | tf_op jit(solution)/shard_map/ppermute | solution.py:247
  290.4 21.3 %collective-permute-done.13 = bf16[512,1024]{1,0:T(8,128)(2,1)S(1)} collective-permute-done((bf16[512,1024]{1,0:T(8,128)(2,1)S(1)}, bf16[512,1024]{1,0:T(8,128)(2,1)S(1)}, u32[]{:S(2)}, u32[]{:S(2)}) %collective-permute-start.13) | collective-permute-done | bytes 1048608 | tf_op jit(solution)/shard_map/ppermute | solution.py:247
  311.7 2.0 multiply_add_fusion.1
  321.9 6.4 %collective-permute-done.16 = bf16[512,512]{1,0:T(8,128)(2,1)S(1)} collective-permute-done((bf16[512,512]{1,0:T(8,128)(2,1)S(1)}, bf16[512,512]{1,0:T(8,128)(2,1)S(1)}, u32[]{:S(2)}, u32[]{:S(2)}) %collective-permute-start.16) | collective-permute-done | bytes 524320 | tf_op jit(solution)/shard_map/ppermute | solution.py:247
  329.7 22.4 %attn_bwd.1 = (bf16[512,1024]{1,0:T(8,128)(2,1)}, bf16[256,1024]{1,0:T(8,128)(2,1)}, bf16[256,1024]{1,0:T(8,128)(2,1)}) custom-call(bf16[512,1024]{1,0:T(8,128)(2,1)} %bitcast.308, bf16[256,1024]{1,0:T(8,128)(2,1)} %bitcast.317, bf16[256,1024]{1,0:T(8,128)(2,1)} %slice.182.refs_2_, bf16[512,1024]{1,0:T(8,128)(2,1)} %pad_maximum_fusion.12.refs_3_, ...), custom_call_target="tpu_custom_call" | custom-call | flops 5368709120 | bytes 7340032 | tf_op jit(solution)/shard_map/attn_bwd/pallas_call | solution.py:177
  358.1 1.8 copy-done.22
  360.0 3.8 convolution_convert_fusion.4
  366.3 3.9 fusion.38
  371.9 1.8 fusion.23
  375.4 2.8 fusion.1
  378.8 2.4 fusion.3
  381.3 2.3 fusion.2
  383.8 4.8 collective-permute-done.25
  388.9 2.1 collective-permute-start.27
  391.0 3.9 collective-permute-done.17
  398.7 1.9 multiply_add_fusion
  402.7 23.8 %collective-permute-done.19 = bf16[4,72,1024]{2,1,0:T(8,128)(2,1)S(1)} collective-permute-done((bf16[4,72,1024]{2,1,0:T(8,128)(2,1)S(1)}, bf16[4,72,1024]{2,1,0:T(8,128)(2,1)S(1)}, u32[]{:S(2)}, u32[]{:S(2)}) %collective-permute-start.19) | collective-permute-done | bytes 589856 | tf_op jit(solution)/shard_map/ppermute | solution.py:235
  426.9 2.1 collective-permute-start.21
  429.0 2.8 collective-permute-start.22
  432.6 2.0 collective-permute-done.20
  440.0 2.9 collective-permute-start.44
  442.8 1.9 collective-permute-start.45
  444.8 7.0 %collective-permute-done.31 = bf16[4,64,2304]{2,1,0:T(8,128)(2,1)S(1)} collective-permute-done((bf16[4,64,2304]{2,1,0:T(8,128)(2,1)S(1)}, bf16[4,64,2304]{2,1,0:T(8,128)(2,1)S(1)}, u32[]{:S(2)}, u32[]{:S(2)}) %collective-permute-start.31) | collective-permute-done | bytes 1179680 | tf_op jit(solution)/shard_map/ppermute | solution.py:235
  452.2 23.2 %collective-permute-done.37 = bf16[4,64,2304]{2,1,0:T(8,128)(2,1)S(1)} collective-permute-done((bf16[4,64,2304]{2,1,0:T(8,128)(2,1)S(1)}, bf16[4,64,2304]{2,1,0:T(8,128)(2,1)S(1)}, u32[]{:S(2)}, u32[]{:S(2)}) %collective-permute-start.37) | collective-permute-done | bytes 1179680 | tf_op jit(solution)/shard_map/ppermute | solution.py:235
  475.9 1.9 collective-permute-start.33
  479.9 3.0 collective-permute-start.34
  485.3 1.9 collective-permute-done.32
  488.2 11.7 %collective-permute-done.33 = bf16[64,2304]{1,0:T(8,128)(2,1)S(1)} collective-permute-done((bf16[64,2304]{1,0:T(8,128)(2,1)S(1)}, bf16[64,2304]{1,0:T(8,128)(2,1)S(1)}, u32[]{:S(2)}, u32[]{:S(2)}) %collective-permute-start.33) | collective-permute-done | bytes 294944 | tf_op jit(solution)/shard_map/ppermute | solution.py:239
  503.5 2.7 collective-permute-done.38
  506.2 16.5 %collective-permute-done.39 = bf16[64,2304]{1,0:T(8,128)(2,1)S(1)} collective-permute-done((bf16[64,2304]{1,0:T(8,128)(2,1)S(1)}, bf16[64,2304]{1,0:T(8,128)(2,1)S(1)}, u32[]{:S(2)}, u32[]{:S(2)}) %collective-permute-start.39) | collective-permute-done | bytes 294944 | tf_op jit(solution)/shard_map/ppermute | solution.py:239
  526.8 2.6 stack.179
  529.4 3.8 convert_bitcast_fusion.1
  535.1 2.9 reshape.382
  538.0 2.2 bitcast_convert_fusion
  540.2 1.8 broadcast_select_fusion.3
  543.6 3.0 stack.181
  546.5 3.9 convert_bitcast_fusion
  550.4 3.8 reshape.386
  554.2 3.6 broadcast_multiply_fusion
  (352 shorter events, 108.7 us)
Async XLA Ops:
  7.2 172.8 %all-gather.6.cloned.1.call-start = ((), (), s32[]{:S(2)}) async-start(), calls=%async_computation.1 | async-start | bytes 5013504 | tf_op jit(solution)/shard_map/all_gather | solution.py:383
  9.0 193.0 %all-gather.4.cloned.1.call-start = ((), (), s32[]{:S(2)}) async-start(), calls=%async_computation | async-start | bytes 10027008 | tf_op jit(solution)/shard_map/all_gather | solution.py:382
  22.3 14.4 %copy-start.2 = (f32[512,1024]{1,0:T(8,128)S(1)}, f32[512,1024]{1,0:T(8,128)}, u32[]{:S(2)}) copy-start(f32[512,1024]{1,0:T(8,128)} %param.14) | copy-start | bytes 6291460
  24.6 14.4 %collective-permute-start.7 = (bf16[64,1024]{1,0:T(8,128)(2,1)}, bf16[64,1024]{1,0:T(8,128)(2,1)}, u32[]{:S(2)}, u32[]{:S(2)}) collective-permute-start(bf16[64,1024]{1,0:T(8,128)(2,1)} %param.22), channel_id=1, source_target_pairs={{0,24},{2,26},{4,28},{6,30},{8,0},{10,2},{12,4},{14,6},{16,8},{18,... | collective-permute-start | bytes 393224 | tf_op jit(solution)/shard_map/ppermute | solution.py:215
  29.8 16.9 %collective-permute-start.8 = (bf16[64,1024]{1,0:T(8,128)(2,1)}, bf16[64,1024]{1,0:T(8,128)(2,1)}, u32[]{:S(2)}, u32[]{:S(2)}) collective-permute-start(bf16[64,1024]{1,0:T(8,128)(2,1)} %param.22), channel_id=1, source_target_pairs={{0,16},{2,18},{4,20},{6,22},{8,24},{10,26},{12,28},{14,30},{16,0},... | collective-permute-start | bytes 393224 | tf_op jit(solution)/shard_map/ppermute | solution.py:215
  29.8 19.3 %collective-permute-start.9 = (bf16[64,1024]{1,0:T(8,128)(2,1)}, bf16[64,1024]{1,0:T(8,128)(2,1)}, u32[]{:S(2)}, u32[]{:S(2)}) collective-permute-start(bf16[64,1024]{1,0:T(8,128)(2,1)} %param.22), channel_id=1, source_target_pairs={{0,8},{2,10},{4,12},{6,14},{8,16},{10,18},{12,20},{14,22},{16,24},... | collective-permute-start | bytes 393224 | tf_op jit(solution)/shard_map/ppermute | solution.py:215
  32.0 18.0 %collective-permute-start = (bf16[72,1024]{1,0:T(8,128)(2,1)}, bf16[72,1024]{1,0:T(8,128)(2,1)S(1)}, u32[]{:S(2)}, u32[]{:S(2)}) collective-permute-start(bf16[72,1024]{1,0:T(8,128)(2,1)} %fusion.57), channel_id=1, source_target_pairs={{0,24},{2,26},{4,28},{6,30},{8,0},{10,2},{12,4},{14,6},{16,8},{18,... | collective-permute-start | bytes 442376 | tf_op jit(solution)/shard_map/ppermute | solution.py:215
  34.8 39.3 %collective-permute-start.1 = (bf16[72,1024]{1,0:T(8,128)(2,1)}, bf16[72,1024]{1,0:T(8,128)(2,1)S(1)}, u32[]{:S(2)}, u32[]{:S(2)}) collective-permute-start(bf16[72,1024]{1,0:T(8,128)(2,1)} %fusion.57), channel_id=1, source_target_pairs={{0,16},{2,18},{4,20},{6,22},{8,24},{10,26},{12,28},{14,30},{16,0},... | collective-permute-start | bytes 442376 | tf_op jit(solution)/shard_map/ppermute | solution.py:215
  37.0 72.9 %copy-start.40 = (f32[512]{0:T(512)}, f32[512]{0:T(512)S(1)}, u32[]{:S(2)}) copy-start(f32[512]{0:T(512)S(1)} %add_rsqrt_fusion.3) | copy-start | bytes 6148
  39.1 35.0 %collective-permute-start.2 = (bf16[72,1024]{1,0:T(8,128)(2,1)}, bf16[72,1024]{1,0:T(8,128)(2,1)S(1)}, u32[]{:S(2)}, u32[]{:S(2)}) collective-permute-start(bf16[72,1024]{1,0:T(8,128)(2,1)} %fusion.57), channel_id=1, source_target_pairs={{0,8},{2,10},{4,12},{6,14},{8,16},{10,18},{12,20},{14,22},{16,24},... | collective-permute-start | bytes 442376 | tf_op jit(solution)/shard_map/ppermute | solution.py:215
  46.7 63.2 %collective-permute-start.5 = (bf16[512,1024]{1,0:T(8,128)(2,1)}, bf16[512,1024]{1,0:T(8,128)(2,1)}, u32[]{:S(2)}, u32[]{:S(2)}) collective-permute-start(bf16[512,1024]{1,0:T(8,128)(2,1)} %multiply_convert_fusion.4), channel_id=1, source_target_pairs={{0,1},{1,0},{2,3},{3,2},{4,5},{5,4},{6,7},{7,6},{8,9},{9,8},{10,11... | collective-permute-start | bytes 3145736 | tf_op jit(solution)/shard_map/ppermute | solution.py:247
  74.2 16.3 %collective-permute-start.3 = (bf16[4,72,1024]{2,1,0:T(8,128)(2,1)S(1)}, bf16[4,72,1024]{2,1,0:T(8,128)(2,1)S(1)}, u32[]{:S(2)}, u32[]{:S(2)}) collective-permute-start(bf16[4,72,1024]{2,1,0:T(8,128)(2,1)S(1)} %constant_dynamic-slice_fusion.6), channel_id=1, source_target_pairs={{0,4},{2,6},{4,0},{6,2},{8,12},{10,14},{12,8},{14,10},{16,20},{18,... | collective-permute-start | bytes 1769480 | tf_op jit(solution)/shard_map/ppermute | solution.py:219
  79.7 27.0 %collective-permute-start.10 = (bf16[4,64,1024]{2,1,0:T(8,128)(2,1)}, bf16[4,64,1024]{2,1,0:T(8,128)(2,1)}, u32[]{:S(2)}, u32[]{:S(2)}) collective-permute-start(bf16[4,64,1024]{2,1,0:T(8,128)(2,1)} %constant_dynamic-slice_fusion.4), channel_id=1, source_target_pairs={{0,4},{2,6},{4,0},{6,2},{8,12},{10,14},{12,8},{14,10},{16,20},{18,... | collective-permute-start | bytes 1572872 | tf_op jit(solution)/shard_map/ppermute | solution.py:219
  91.7 21.1 %collective-permute-start.4 = (bf16[4,2,72,1024]{3,2,1,0:T(8,128)(2,1)}, bf16[4,2,72,1024]{3,2,1,0:T(8,128)(2,1)}, u32[]{:S(2)}, u32[]{:S(2)}) collective-permute-start(bf16[4,2,72,1024]{3,2,1,0:T(8,128)(2,1)} %pad_maximum_fusion.9), channel_id=1, source_target_pairs={{0,2},{2,0},{4,6},{6,4},{8,10},{10,8},{12,14},{14,12},{16,18},{18,... | collective-permute-start | bytes 3538952 | tf_op jit(solution)/shard_map/ppermute | solution.py:221
  109.8 36.7 %collective-permute-start.11 = (bf16[4,2,64,1024]{3,2,1,0:T(8,128)(2,1)}, bf16[4,2,64,1024]{3,2,1,0:T(8,128)(2,1)}, u32[]{:S(2)}, u32[]{:S(2)}) collective-permute-start(bf16[4,2,64,1024]{3,2,1,0:T(8,128)(2,1)} %pad_maximum_fusion.11), channel_id=1, source_target_pairs={{0,2},{2,0},{4,6},{6,4},{8,10},{10,8},{12,14},{14,12},{16,18},{18,... | collective-permute-start | bytes 3145736 | tf_op jit(solution)/shard_map/ppermute | solution.py:221
  142.5 14.9 %collective-permute-start.6 = (bf16[512,512]{1,0:T(8,128)(2,1)S(1)}, bf16[512,512]{1,0:T(8,128)(2,1)S(1)}, u32[]{:S(2)}, u32[]{:S(2)}) collective-permute-start(bf16[512,512]{1,0:T(8,128)(2,1)S(1)} %constant_dynamic-slice_fusion.5), channel_id=1, source_target_pairs={{0,1},{1,0},{2,3},{3,2},{4,5},{5,4},{6,7},{7,6},{8,9},{9,8},{10,11... | collective-permute-start | bytes 1572872 | tf_op jit(solution)/shard_map/ppermute | solution.py:247
  145.8 34.1 %collective-permute-start.14 = (bf16[512,1024]{1,0:T(8,128)(2,1)S(1)}, bf16[512,1024]{1,0:T(8,128)(2,1)}, u32[]{:S(2)}, u32[]{:S(2)}) collective-permute-start(bf16[512,1024]{1,0:T(8,128)(2,1)S(1)} %convert_element_type.416), channel_id=1, source_target_pairs={{0,1},{1,0},{2,3},{3,2},{4,5},{5,4},{6,7},{7,6},{8,9},{9,8},{10,11... | collective-permute-start | bytes 3145736 | tf_op jit(solution)/shard_map/ppermute | solution.py:247
  161.7 40.3 %collective-permute-start.12 = (bf16[512,1024]{1,0:T(8,128)(2,1)}, bf16[512,1024]{1,0:T(8,128)(2,1)}, u32[]{:S(2)}, u32[]{:S(2)}) collective-permute-start(bf16[512,1024]{1,0:T(8,128)(2,1)} %multiply_convert_fusion.3), channel_id=1, source_target_pairs={{0,1},{1,0},{2,3},{3,2},{4,5},{5,4},{6,7},{7,6},{8,9},{9,8},{10,11... | collective-permute-start | bytes 3145736 | tf_op jit(solution)/shard_map/ppermute | solution.py:247
  230.5 11.5 %copy-start.50 = (bf16[1024,2304]{1,0:T(8,128)(2,1)S(1)}, bf16[1024,2304]{1,0:T(8,128)(2,1)}, u32[]{:S(2)}) copy-start(bf16[1024,2304]{1,0:T(8,128)(2,1)} %get-tuple-element.25) | copy-start | bytes 14155780
  238.5 14.9 %slice-start.4 = ((s8[9437184]{0:T(1024)(128)(4,1)}), s8[4194304]{0:T(1024)(128)(4,1)S(1)}, s32[]{:S(2)}) async-start(s8[9437184]{0:T(1024)(128)(4,1)} %bitcast.320), calls=%async_computation.6 | async-start | bytes 8388608
  238.5 14.9 %slice-start.9 = ((s8[4718592]{0:T(1024)(128)(4,1)}), s8[4194304]{0:T(1024)(128)(4,1)S(1)}, s32[]{:S(2)}) async-start(s8[4718592]{0:T(1024)(128)(4,1)} %bitcast.324), calls=%async_computation.11 | async-start | bytes 8388608
  242.0 131.7 %collective-permute-start.42 = (bf16[4,2,144,1024]{3,2,1,0:T(8,128)(2,1)}, bf16[4,2,144,1024]{3,2,1,0:T(8,128)(2,1)}, u32[]{:S(2)}, u32[]{:S(2)}) collective-permute-start(bf16[4,2,144,1024]{3,2,1,0:T(8,128)(2,1)} %dynamic-slice_bitcast_fusion), channel_id=1, source_target_pairs={{0,2},{2,0},{4,6},{6,4},{8,10},{10,8},{12,14},{14,12},{16,18},{18,... | collective-permute-start | bytes 7077896 | tf_op jit(solution)/shard_map/ppermute | solution.py:233
  242.0 11.4 %slice-start.5 = ((s8[9437184]{0:T(1024)(128)(4,1)}), s8[4194304]{0:T(1024)(128)(4,1)S(1)}, s32[]{:S(2)}) async-start(s8[9437184]{0:T(1024)(128)(4,1)} %bitcast.320), calls=%async_computation.7 | async-start | bytes 8388608
  242.1 11.4 %slice-start.6 = ((s8[9437184]{0:T(1024)(128)(4,1)}), s8[1048576]{0:T(1024)(128)(4,1)S(1)}, s32[]{:S(2)}) async-start(s8[9437184]{0:T(1024)(128)(4,1)} %bitcast.320), calls=%async_computation.8 | async-start | bytes 2097152
  242.1 11.4 %slice-start.10 = ((s8[4718592]{0:T(1024)(128)(4,1)}), s8[524288]{0:T(1024)(128)(4,1)S(1)}, s32[]{:S(2)}) async-start(s8[4718592]{0:T(1024)(128)(4,1)} %bitcast.324), calls=%async_computation.12 | async-start | bytes 1048576
  253.2 125.1 %collective-permute-start.30 = (bf16[4,2,64,2304]{3,2,1,0:T(8,128)(2,1)}, bf16[4,2,64,2304]{3,2,1,0:T(8,128)(2,1)}, u32[]{:S(2)}, u32[]{:S(2)}) collective-permute-start(bf16[4,2,64,2304]{3,2,1,0:T(8,128)(2,1)} %dynamic-slice_bitcast_fusion.1), channel_id=1, source_target_pairs={{0,2},{2,0},{4,6},{6,4},{8,10},{10,8},{12,14},{14,12},{16,18},{18,... | collective-permute-start | bytes 7077896 | tf_op jit(solution)/shard_map/ppermute | solution.py:233
  253.5 11.9 %slice-start.7 = ((s8[4718592]{0:T(1024)(128)(4,1)}), s8[4194304]{0:T(1024)(128)(4,1)S(1)}, s32[]{:S(2)}) async-start(s8[4718592]{0:T(1024)(128)(4,1)} %bitcast.322), calls=%async_computation.9 | async-start | bytes 8388608
  263.8 26.1 %collective-permute-start.15 = (bf16[512,1024]{1,0:T(8,128)(2,1)S(1)}, bf16[512,1024]{1,0:T(8,128)(2,1)S(1)}, u32[]{:S(2)}, u32[]{:S(2)}) collective-permute-start(bf16[512,1024]{1,0:T(8,128)(2,1)S(1)} %slice.180), channel_id=1, source_target_pairs={{0,1},{1,0},{2,3},{3,2},{4,5},{5,4},{6,7},{7,6},{8,9},{9,8},{10,11... | collective-permute-start | bytes 3145736 | tf_op jit(solution)/shard_map/ppermute | solution.py:247
  272.4 17.5 %copy-start.6 = (f32[512,1024]{1,0:T(8,128)S(1)}, f32[512,1024]{1,0:T(8,128)}, u32[]{:S(2)}) copy-start(f32[512,1024]{1,0:T(8,128)} %copy-done.5) | copy-start | bytes 6291460
  272.4 39.2 %collective-permute-start.13 = (bf16[512,1024]{1,0:T(8,128)(2,1)S(1)}, bf16[512,1024]{1,0:T(8,128)(2,1)S(1)}, u32[]{:S(2)}, u32[]{:S(2)}) collective-permute-start(bf16[512,1024]{1,0:T(8,128)(2,1)S(1)} %slice.181), channel_id=1, source_target_pairs={{0,1},{1,0},{2,3},{3,2},{4,5},{5,4},{6,7},{7,6},{8,9},{9,8},{10,11... | collective-permute-start | bytes 3145736 | tf_op jit(solution)/shard_map/ppermute | solution.py:247
  281.1 30.6 %copy-start.9 = (f32[512,1024]{1,0:T(8,128)S(1)}, f32[512,1024]{1,0:T(8,128)}, u32[]{:S(2)}) copy-start(f32[512,1024]{1,0:T(8,128)} %param.27) | copy-start | bytes 6291460
  290.4 23.3 %copy-start.24 = (bf16[4,2,2,64,1024]{4,3,2,1,0:T(8,128)(2,1)S(1)}, bf16[4,2,2,64,1024]{4,3,2,1,0:T(8,128)(2,1)}, u32[]{:S(2)}) copy-start(bf16[4,2,2,64,1024]{4,3,2,1,0:T(8,128)(2,1)} %copy-done.23) | copy-start | bytes 6291460
  315.0 13.3 %collective-permute-start.16 = (bf16[512,512]{1,0:T(8,128)(2,1)S(1)}, bf16[512,512]{1,0:T(8,128)(2,1)S(1)}, u32[]{:S(2)}, u32[]{:S(2)}) collective-permute-start(bf16[512,512]{1,0:T(8,128)(2,1)S(1)} %constant_dynamic-slice_fusion.2), channel_id=1, source_target_pairs={{0,1},{1,0},{2,3},{3,2},{4,5},{5,4},{6,7},{7,6},{8,9},{9,8},{10,11... | collective-permute-start | bytes 1572872 | tf_op jit(solution)/shard_map/ppermute | solution.py:247
  319.9 61.4 %collective-permute-start.36 = (bf16[4,2,64,2304]{3,2,0,1:T(8,128)(2,1)}, bf16[4,2,64,2304]{3,2,0,1:T(8,128)(2,1)}, u32[]{:S(2)}, u32[]{:S(2)}) collective-permute-start(bf16[4,2,64,2304]{3,2,0,1:T(8,128)(2,1)} %bitcast.282), channel_id=1, source_target_pairs={{0,2},{2,0},{4,6},{6,4},{8,10},{10,8},{12,14},{14,12},{16,18},{18,... | collective-permute-start | bytes 7077896 | tf_op jit(solution)/shard_map/ppermute | solution.py:233
  321.3 49.0 %collective-permute-start.24 = (bf16[4,2,64,1024]{3,2,1,0:T(8,128)(2,1)S(1)}, bf16[4,2,64,1024]{3,2,1,0:T(8,128)(2,1)}, u32[]{:S(2)}, u32[]{:S(2)}) collective-permute-start(bf16[4,2,64,1024]{3,2,1,0:T(8,128)(2,1)S(1)} %dynamic-slice_bitcast_fusion.5), channel_id=1, source_target_pairs={{0,2},{2,0},{4,6},{6,4},{8,10},{10,8},{12,14},{14,12},{16,18},{18,... | collective-permute-start | bytes 3145736 | tf_op jit(solution)/shard_map/ppermute | solution.py:233
  364.1 11.3 %slice-start.2 = ((s8[4718592]{0:T(1024)(128)(4,1)}), s8[4194304]{0:T(1024)(128)(4,1)S(1)}, s32[]{:S(2)}) async-start(s8[4718592]{0:T(1024)(128)(4,1)} %bitcast.295), calls=%async_computation.4 | async-start | bytes 8388608
  365.6 30.1 %collective-permute-start.18 = (bf16[4,2,72,1024]{3,2,1,0:T(8,128)(2,1)S(1)}, bf16[4,2,72,1024]{3,2,1,0:T(8,128)(2,1)S(1)}, u32[]{:S(2)}, u32[]{:S(2)}) collective-permute-start(bf16[4,2,72,1024]{3,2,1,0:T(8,128)(2,1)S(1)} %fusion.30), channel_id=1, source_target_pairs={{0,2},{2,0},{4,6},{6,4},{8,10},{10,8},{12,14},{14,12},{16,18},{18,... | collective-permute-start | bytes 3538952 | tf_op jit(solution)/shard_map/ppermute | solution.py:233
  370.4 24.6 %collective-permute-start.17 = (bf16[512,1024]{1,0:T(8,128)(2,1)S(1)}, bf16[512,1024]{1,0:T(8,128)(2,1)S(1)}, u32[]{:S(2)}, u32[]{:S(2)}) collective-permute-start(bf16[512,1024]{1,0:T(8,128)(2,1)S(1)} %dynamic-slice_convert_fusion), channel_id=1, source_target_pairs={{0,1},{1,0},{2,3},{3,2},{4,5},{5,4},{6,7},{7,6},{8,9},{9,8},{10,11... | collective-permute-start | bytes 3145736 | tf_op jit(solution)/shard_map/ppermute | solution.py:247
  373.8 14.9 %collective-permute-start.25 = (bf16[4,64,1024]{2,1,0:T(8,128)(2,1)S(1)}, bf16[4,64,1024]{2,1,0:T(8,128)(2,1)S(1)}, u32[]{:S(2)}, u32[]{:S(2)}) collective-permute-start(bf16[4,64,1024]{2,1,0:T(8,128)(2,1)S(1)} %dynamic-slice_bitcast_fusion.7), channel_id=1, source_target_pairs={{0,4},{2,6},{4,0},{6,2},{8,12},{10,14},{12,8},{14,10},{16,20},{18,... | collective-permute-start | bytes 1572872 | tf_op jit(solution)/shard_map/ppermute | solution.py:235
  378.3 61.1 %collective-permute-start.43 = (bf16[4,144,1024]{2,1,0:T(8,128)(2,1)S(1)}, bf16[4,144,1024]{2,1,0:T(8,128)(2,1)S(1)}, u32[]{:S(2)}, u32[]{:S(2)}) collective-permute-start(bf16[4,144,1024]{2,1,0:T(8,128)(2,1)S(1)} %dynamic-slice_bitcast_fusion.2), channel_id=1, source_target_pairs={{0,4},{2,6},{4,0},{6,2},{8,12},{10,14},{12,8},{14,10},{16,20},{18,... | collective-permute-start | bytes 3538952 | tf_op jit(solution)/shard_map/ppermute | solution.py:235
  383.7 11.5 %copy-start.41 = (f32[512]{0:T(512)S(1)}, f32[512]{0:T(512)}, u32[]{:S(2)}) copy-start(f32[512]{0:T(512)} %copy-done.40) | copy-start | bytes 6148
  388.9 11.8 %collective-permute-start.26 = (bf16[64,1024]{1,0:T(8,128)(2,1)S(1)}, bf16[64,1024]{1,0:T(8,128)(2,1)S(1)}, u32[]{:S(2)}, u32[]{:S(2)}) collective-permute-start(bf16[64,1024]{1,0:T(8,128)(2,1)S(1)} %get-tuple-element.83), channel_id=1, source_target_pairs={{0,8},{2,10},{4,12},{6,14},{8,16},{10,18},{12,20},{14,22},{16,24},... | collective-permute-start | bytes 393224 | tf_op jit(solution)/shard_map/ppermute | solution.py:239
  388.9 12.2 %collective-permute-start.27 = (bf16[64,1024]{1,0:T(8,128)(2,1)S(1)}, bf16[64,1024]{1,0:T(8,128)(2,1)S(1)}, u32[]{:S(2)}, u32[]{:S(2)}) collective-permute-start(bf16[64,1024]{1,0:T(8,128)(2,1)S(1)} %get-tuple-element.85), channel_id=1, source_target_pairs={{0,16},{2,18},{4,20},{6,22},{8,24},{10,26},{12,28},{14,30},{16,0},... | collective-permute-start | bytes 393224 | tf_op jit(solution)/shard_map/ppermute | solution.py:239
  395.0 6.2 %collective-permute-start.28 = (bf16[64,1024]{1,0:T(8,128)(2,1)S(1)}, bf16[64,1024]{1,0:T(8,128)(2,1)S(1)}, u32[]{:S(2)}, u32[]{:S(2)}) collective-permute-start(bf16[64,1024]{1,0:T(8,128)(2,1)S(1)} %get-tuple-element.84), channel_id=1, source_target_pairs={{0,24},{2,26},{4,28},{6,30},{8,0},{10,2},{12,4},{14,6},{16,8},{18,... | collective-permute-start | bytes 393224 | tf_op jit(solution)/shard_map/ppermute | solution.py:239
  397.1 29.4 %collective-permute-start.19 = (bf16[4,72,1024]{2,1,0:T(8,128)(2,1)S(1)}, bf16[4,72,1024]{2,1,0:T(8,128)(2,1)S(1)}, u32[]{:S(2)}, u32[]{:S(2)}) collective-permute-start(bf16[4,72,1024]{2,1,0:T(8,128)(2,1)S(1)} %dynamic-slice_bitcast_fusion.6), channel_id=1, source_target_pairs={{0,4},{2,6},{4,0},{6,2},{8,12},{10,14},{12,8},{14,10},{16,20},{18,... | collective-permute-start | bytes 1769480 | tf_op jit(solution)/shard_map/ppermute | solution.py:235
  400.6 51.2 %collective-permute-start.31 = (bf16[4,64,2304]{2,1,0:T(8,128)(2,1)S(1)}, bf16[4,64,2304]{2,1,0:T(8,128)(2,1)S(1)}, u32[]{:S(2)}, u32[]{:S(2)}) collective-permute-start(bf16[4,64,2304]{2,1,0:T(8,128)(2,1)S(1)} %dynamic-slice_bitcast_fusion.4), channel_id=1, source_target_pairs={{0,4},{2,6},{4,0},{6,2},{8,12},{10,14},{12,8},{14,10},{16,20},{18,... | collective-permute-start | bytes 3538952 | tf_op jit(solution)/shard_map/ppermute | solution.py:235
  401.2 27.8 %collective-permute-start.29 = (bf16[64,1024]{1,0:T(8,128)(2,1)S(1)}, bf16[64,1024]{1,0:T(8,128)(2,1)S(1)}, u32[]{:S(2)}, u32[]{:S(2)}) collective-permute-start(bf16[64,1024]{1,0:T(8,128)(2,1)S(1)} %fusion.56), channel_id=1, source_target_pairs={{0,1},{1,0},{2,3},{3,2},{4,5},{5,4},{6,7},{7,6},{8,9},{9,8},{10,11... | collective-permute-start | bytes 393224 | tf_op jit(solution)/shard_map/ppermute | solution.py:247
  426.8 7.8 %collective-permute-start.20 = (bf16[72,1024]{1,0:T(8,128)(2,1)S(1)}, bf16[72,1024]{1,0:T(8,128)(2,1)S(1)}, u32[]{:S(2)}, u32[]{:S(2)}) collective-permute-start(bf16[72,1024]{1,0:T(8,128)(2,1)S(1)} %get-tuple-element.80), channel_id=1, source_target_pairs={{0,8},{2,10},{4,12},{6,14},{8,16},{10,18},{12,20},{14,22},{16,24},... | collective-permute-start | bytes 442376 | tf_op jit(solution)/shard_map/ppermute | solution.py:239
  426.9 10.8 %collective-permute-start.21 = (bf16[72,1024]{1,0:T(8,128)(2,1)S(1)}, bf16[72,1024]{1,0:T(8,128)(2,1)S(1)}, u32[]{:S(2)}, u32[]{:S(2)}) collective-permute-start(bf16[72,1024]{1,0:T(8,128)(2,1)S(1)} %get-tuple-element.82), channel_id=1, source_target_pairs={{0,16},{2,18},{4,20},{6,22},{8,24},{10,26},{12,28},{14,30},{16,0},... | collective-permute-start | bytes 442376 | tf_op jit(solution)/shard_map/ppermute | solution.py:239
  429.0 8.8 %collective-permute-start.22 = (bf16[72,1024]{1,0:T(8,128)(2,1)S(1)}, bf16[72,1024]{1,0:T(8,128)(2,1)S(1)}, u32[]{:S(2)}, u32[]{:S(2)}) collective-permute-start(bf16[72,1024]{1,0:T(8,128)(2,1)S(1)} %get-tuple-element.81), channel_id=1, source_target_pairs={{0,24},{2,26},{4,28},{6,30},{8,0},{10,2},{12,4},{14,6},{16,8},{18,... | collective-permute-start | bytes 442376 | tf_op jit(solution)/shard_map/ppermute | solution.py:239
  434.6 40.9 %collective-permute-start.37 = (bf16[4,64,2304]{2,1,0:T(8,128)(2,1)S(1)}, bf16[4,64,2304]{2,1,0:T(8,128)(2,1)S(1)}, u32[]{:S(2)}, u32[]{:S(2)}) collective-permute-start(bf16[4,64,2304]{2,1,0:T(8,128)(2,1)S(1)} %dynamic-slice_bitcast_fusion.3), channel_id=1, source_target_pairs={{0,4},{2,6},{4,0},{6,2},{8,12},{10,14},{12,8},{14,10},{16,20},{18,... | collective-permute-start | bytes 3538952 | tf_op jit(solution)/shard_map/ppermute | solution.py:235
  437.8 38.0 %collective-permute-start.23 = (bf16[72,1024]{1,0:T(8,128)(2,1)S(1)}, bf16[72,1024]{1,0:T(8,128)(2,1)S(1)}, u32[]{:S(2)}, u32[]{:S(2)}) collective-permute-start(bf16[72,1024]{1,0:T(8,128)(2,1)S(1)} %fusion.52), channel_id=1, source_target_pairs={{0,1},{1,0},{2,3},{3,2},{4,5},{5,4},{6,7},{7,6},{8,9},{9,8},{10,11... | collective-permute-start | bytes 442376 | tf_op jit(solution)/shard_map/ppermute | solution.py:247
  440.0 39.9 %collective-permute-start.44 = (bf16[144,1024]{1,0:T(8,128)(2,1)S(1)}, bf16[144,1024]{1,0:T(8,128)(2,1)S(1)}, u32[]{:S(2)}, u32[]{:S(2)}) collective-permute-start(bf16[144,1024]{1,0:T(8,128)(2,1)S(1)} %get-tuple-element.56), channel_id=1, source_target_pairs={{0,8},{2,10},{4,12},{6,14},{8,16},{10,18},{12,20},{14,22},{16,24},... | collective-permute-start | bytes 884744 | tf_op jit(solution)/shard_map/ppermute | solution.py:239
  442.8 41.1 %collective-permute-start.45 = (bf16[144,1024]{1,0:T(8,128)(2,1)S(1)}, bf16[144,1024]{1,0:T(8,128)(2,1)S(1)}, u32[]{:S(2)}, u32[]{:S(2)}) collective-permute-start(bf16[144,1024]{1,0:T(8,128)(2,1)S(1)} %get-tuple-element.58), channel_id=1, source_target_pairs={{0,16},{2,18},{4,20},{6,22},{8,24},{10,26},{12,28},{14,30},{16,0},... | collective-permute-start | bytes 884744 | tf_op jit(solution)/shard_map/ppermute | solution.py:239
  451.8 32.1 %collective-permute-start.46 = (bf16[144,1024]{1,0:T(8,128)(2,1)S(1)}, bf16[144,1024]{1,0:T(8,128)(2,1)S(1)}, u32[]{:S(2)}, u32[]{:S(2)}) collective-permute-start(bf16[144,1024]{1,0:T(8,128)(2,1)S(1)} %get-tuple-element.57), channel_id=1, source_target_pairs={{0,24},{2,26},{4,28},{6,30},{8,0},{10,2},{12,4},{14,6},{16,8},{18,... | collective-permute-start | bytes 884744 | tf_op jit(solution)/shard_map/ppermute | solution.py:239
  475.5 11.7 %collective-permute-start.32 = (bf16[64,2304]{1,0:T(8,128)(2,1)S(1)}, bf16[64,2304]{1,0:T(8,128)(2,1)S(1)}, u32[]{:S(2)}, u32[]{:S(2)}) collective-permute-start(bf16[64,2304]{1,0:T(8,128)(2,1)S(1)} %get-tuple-element.62), channel_id=1, source_target_pairs={{0,8},{2,10},{4,12},{6,14},{8,16},{10,18},{12,20},{14,22},{16,24},... | collective-permute-start | bytes 884744 | tf_op jit(solution)/shard_map/ppermute | solution.py:239
  475.9 24.0 %collective-permute-start.33 = (bf16[64,2304]{1,0:T(8,128)(2,1)S(1)}, bf16[64,2304]{1,0:T(8,128)(2,1)S(1)}, u32[]{:S(2)}, u32[]{:S(2)}) collective-permute-start(bf16[64,2304]{1,0:T(8,128)(2,1)S(1)} %get-tuple-element.64), channel_id=1, source_target_pairs={{0,16},{2,18},{4,20},{6,22},{8,24},{10,26},{12,28},{14,30},{16,0},... | collective-permute-start | bytes 884744 | tf_op jit(solution)/shard_map/ppermute | solution.py:239
  479.9 22.0 %collective-permute-start.34 = (bf16[64,2304]{1,0:T(8,128)(2,1)S(1)}, bf16[64,2304]{1,0:T(8,128)(2,1)S(1)}, u32[]{:S(2)}, u32[]{:S(2)}) collective-permute-start(bf16[64,2304]{1,0:T(8,128)(2,1)S(1)} %get-tuple-element.63), channel_id=1, source_target_pairs={{0,24},{2,26},{4,28},{6,30},{8,0},{10,2},{12,4},{14,6},{16,8},{18,... | collective-permute-start | bytes 884744 | tf_op jit(solution)/shard_map/ppermute | solution.py:239
  483.9 22.3 %collective-permute-start.38 = (bf16[64,2304]{1,0:T(8,128)(2,1)S(1)}, bf16[64,2304]{1,0:T(8,128)(2,1)S(1)}, u32[]{:S(2)}, u32[]{:S(2)}) collective-permute-start(bf16[64,2304]{1,0:T(8,128)(2,1)S(1)} %get-tuple-element.65), channel_id=1, source_target_pairs={{0,8},{2,10},{4,12},{6,14},{8,16},{10,18},{12,20},{14,22},{16,24},... | collective-permute-start | bytes 884744 | tf_op jit(solution)/shard_map/ppermute | solution.py:239
  484.0 38.8 %collective-permute-start.39 = (bf16[64,2304]{1,0:T(8,128)(2,1)S(1)}, bf16[64,2304]{1,0:T(8,128)(2,1)S(1)}, u32[]{:S(2)}, u32[]{:S(2)}) collective-permute-start(bf16[64,2304]{1,0:T(8,128)(2,1)S(1)} %get-tuple-element.67), channel_id=1, source_target_pairs={{0,16},{2,18},{4,20},{6,22},{8,24},{10,26},{12,28},{14,30},{16,0},... | collective-permute-start | bytes 884744 | tf_op jit(solution)/shard_map/ppermute | solution.py:239
  487.2 35.5 %collective-permute-start.40 = (bf16[64,2304]{1,0:T(8,128)(2,1)S(1)}, bf16[64,2304]{1,0:T(8,128)(2,1)S(1)}, u32[]{:S(2)}, u32[]{:S(2)}) collective-permute-start(bf16[64,2304]{1,0:T(8,128)(2,1)S(1)} %get-tuple-element.66), channel_id=1, source_target_pairs={{0,24},{2,26},{4,28},{6,30},{8,0},{10,2},{12,4},{14,6},{16,8},{18,... | collective-permute-start | bytes 884744 | tf_op jit(solution)/shard_map/ppermute | solution.py:239
  499.9 33.3 %collective-permute-start.47 = (bf16[144,1024]{1,0:T(8,128)(2,1)S(1)}, bf16[144,1024]{1,0:T(8,128)(2,1)}, u32[]{:S(2)}, u32[]{:S(2)}) collective-permute-start(bf16[144,1024]{1,0:T(8,128)(2,1)S(1)} %fusion.41), channel_id=1, source_target_pairs={{0,1},{1,0},{2,3},{3,2},{4,5},{5,4},{6,7},{7,6},{8,9},{9,8},{10,11... | collective-permute-start | bytes 884744 | tf_op jit(solution)/shard_map/ppermute | solution.py:247
  502.0 23.2 %collective-permute-start.35 = (bf16[64,2304]{1,0:T(8,128)(2,1)S(1)}, bf16[64,2304]{1,0:T(8,128)(2,1)S(1)}, u32[]{:S(2)}, u32[]{:S(2)}) collective-permute-start(bf16[64,2304]{1,0:T(8,128)(2,1)S(1)} %fusion.47), channel_id=1, source_target_pairs={{0,1},{1,0},{2,3},{3,2},{4,5},{5,4},{6,7},{7,6},{8,9},{9,8},{10,11... | collective-permute-start | bytes 884744 | tf_op jit(solution)/shard_map/ppermute | solution.py:247
  523.6 16.6 %collective-permute-start.41 = (bf16[64,2304]{1,0:T(8,128)(2,1)}, bf16[64,2304]{1,0:T(8,128)(2,1)}, u32[]{:S(2)}, u32[]{:S(2)}) collective-permute-start(bf16[64,2304]{1,0:T(8,128)(2,1)} %fusion.44), channel_id=1, source_target_pairs={{0,1},{1,0},{2,3},{3,2},{4,5},{5,4},{6,7},{7,6},{8,9},{9,8},{10,11... | collective-permute-start | bytes 884744 | tf_op jit(solution)/shard_map/ppermute | solution.py:247
  (51 other events, 235.0 us)
Sparse Core Ops, SparseCore 0:
  10.3 69.2 all-gather.5
  81.9 82.3 all-gather.3

commit v2 on v1

--- a/solution.py
+++ b/solution.py
@@ -195,6 +195,159 @@
     )(q, k, v, d_out, out, lse, *extra)
 
 
+def ff_prep_kernel(rank_ref, gate_ref, up_ref, down_ref, gain_ref, out_ref):
+    first = rank_ref[0] == 0
+    d_dp, ff_all = gate_ref.shape
+    ff_w = down_ref.shape[0] // 2
+    dp_n = ff_all // (2 * ff_w)
+    gain = gain_ref[...]
+    for half, ref in enumerate((gate_ref, up_ref)):
+        for i in range(dp_n):
+            lo = ref[:, 2 * i * ff_w : (2 * i + 1) * ff_w].astype(F32)
+            hi = ref[:, (2 * i + 1) * ff_w : (2 * i + 2) * ff_w].astype(F32)
+            at = (half * dp_n + i) * ff_w
+            out_ref[:d_dp, at : at + ff_w] = (jnp.where(first, lo, hi) * gain).astype(BF)
+    for b in range(ff_w // 16):
+        lo = down_ref[16 * b : 16 * b + 16, :]
+        hi = down_ref[ff_w + 16 * b : ff_w + 16 * b + 16, :]
+        rows = jnp.where(first, lo.astype(F32), hi.astype(F32)).astype(BF)
+        for band, at, frm, to in down_places(b, rows.shape[1], ff_all):
+            out_ref[d_dp + 16 * band : d_dp + 16 * band + 16, at : at + to - frm] = rows[:, frm:to]
+
+
+def down_places(b, width, ff_all):
+    places, start = [], b * width
+    while start < (b + 1) * width:
+        band = start // ff_all
+        end = min((band + 1) * ff_all, (b + 1) * width)
+        places.append((band, start - band * ff_all, start - b * width, end - b * width))
+        start = end
+    return places
+
+
+def ff_prep(rank, w_gate, w_up, w_down, gain):
+    d_dp, ff_all = w_gate.shape
+    bands = w_down.shape[0] // 2 * w_down.shape[1] // ff_all
+    whole = lambda arr: pl.BlockSpec(arr.shape, lambda i, r: (0, 0))
+    return pl.pallas_call(
+        ff_prep_kernel,
+        grid_spec=pltpu.PrefetchScalarGridSpec(
+            num_scalar_prefetch=1,
+            grid=(1,),
+            in_specs=[whole(w_gate), whole(w_up), whole(w_down), whole(gain)],
+            out_specs=pl.BlockSpec((d_dp + bands, ff_all), lambda i, r: (0, 0)),
+        ),
+        out_shape=jax.ShapeDtypeStruct((d_dp + bands, ff_all), BF),
+        name="ff_prep",
+    )(rank[None], w_gate, w_up, w_down, gain)
+
+
+def ffn_core_kernel(sub, fresh, *refs):
+    x_ref, g_ref, wg_ref, wu_ref, wd_ref = refs[:5]
+    hid_ref, dg_ref, du_ref, dx_ref, out_ref, down = refs[5:] if fresh else refs[8:]
+    dp_n, d_dp, blk = wg_ref.shape
+    width = g_ref.shape[1]
+    ff_all = wd_ref.shape[2]
+    ff_w = down.shape[0] // dp_n
+    step = pl.program_id(0)
+
+    @pl.when(step == 0)
+    def _():
+        dx_ref[...] = jnp.zeros_like(dx_ref)
+        out_ref[...] = jnp.zeros_like(out_ref)
+
+        @pl.loop(0, dp_n)
+        def _(i):
+            for b in range(ff_w // 16):
+                rows = pl.ds(pl.multiple_of(i * ff_w + 16 * b, 16), 16)
+                for band, at, frm, to in down_places(b, width, ff_all):
+                    down[rows, frm:to] = wd_ref[i, 16 * band : 16 * band + 16, at : at + to - frm]
+
+    @pl.loop(0, blk // sub)
+    def _(s):
+        cols = pl.ds(pl.multiple_of(s * sub, 128), sub)
+        rows = pl.ds(pl.multiple_of(step * blk + s * sub, 128), sub)
+        x = x_ref[...]
+        w_gate = wg_ref[:, :, cols].reshape(dp_n * d_dp, sub)
+        w_up = wu_ref[:, :, cols].reshape(dp_n * d_dp, sub)
+        w_down = down[rows, :]
+        gate = dot(x, w_gate, 1, 0)
+        up = dot(x, w_up, 1, 0)
+        d_hid = dot(g_ref[...], w_down, 1, 1)
+        sig = 1.0 / (1.0 + jnp.exp(-gate))
+        silu = gate * sig
+        hidden = (silu * up).astype(BF)
+        d_gate = (d_hid * up * (sig * (1.0 + gate * (1.0 - sig)))).astype(BF)
+        d_up = (d_hid * silu).astype(BF)
+        hid_ref[:, cols] = hidden
+        dg_ref[:, cols] = d_gate
+        du_ref[:, cols] = d_up
+        dx_ref[...] += dot(d_gate, w_gate, 1, 1) + dot(d_up, w_up, 1, 1)
+        out_ref[...] += dot(hidden, w_down, 1, 0)
+
+
+def ffn_core(x, g, packed, earlier, half, dp_n, d_dp, ff_w):
+    rows, width = x.shape
+    ff = dp_n * ff_w
+    blk = ff // 2
+    fresh = earlier is None
+    whole = pl.BlockSpec((rows, width), lambda j: (0, 0))
+    wide = pl.BlockSpec((rows, blk), lambda j: (half, j))
+    bands = packed.shape[1] - d_dp
+    keep = pl.BlockSpec(memory_space=pl.ANY)
+    wide_shape = jax.ShapeDtypeStruct((2 * rows, ff), BF)
+    return pl.pallas_call(
+        partial(ffn_core_kernel, 384, fresh),
+        grid=(2,),
+        in_specs=[
+            whole,
+            whole,
+            pl.BlockSpec((dp_n, d_dp, blk), lambda j: (0, 0, j)),
+            pl.BlockSpec((dp_n, d_dp, blk), lambda j: (0, 0, 2 + j)),
+            pl.BlockSpec(
+                (dp_n, bands, 2 * ff), lambda j: (0, d_dp // bands, 0), pipeline_mode=pl.Buffered(1)
+            ),
+        ]
+        + ([] if fresh else [keep] * 3),
+        out_specs=[wide, wide, wide, whole, whole],
+        out_shape=[wide_shape] * 3 + [jax.ShapeDtypeStruct((rows, width), F32)] * 2,
+        scratch_shapes=[pltpu.VMEM((ff, width), BF)],
+        input_output_aliases={} if fresh else {5: 0, 6: 1, 7: 2},
+        compiler_params=pltpu.CompilerParams(vmem_limit_bytes=60 << 20),
+        cost_estimate=pl.CostEstimate(
+            flops=12 * rows * width * ff,
+            transcendentals=rows * ff,
+            bytes_accessed=6 * width * ff + 6 * rows * ff + 12 * rows * width,
+        ),
+        name="ffn_core",
+    )(x, g, packed, packed, packed, *(() if fresh else earlier))
+
+
+def assemble_kernel(place_ref, *refs):
+    out_ref = refs[-1]
+    rows = refs[0].shape[0]
+    z, x, core = place_ref[0], place_ref[1], place_ref[2]
+    for n, ref in enumerate(refs[:-1]):
+        b, a, s = n // 8, n // 4 % 2, n % 4
+        at = (lax.rem(z + s, 4) * 2 + (a + x - 2 * a * x)) * 2 + (b + core - 2 * b * core)
+        out_ref[at] = ref[...]
+
+
+def assemble(place, pieces):
+    shape = pieces[0].shape
+    return pl.pallas_call(
+        assemble_kernel,
+        grid_spec=pltpu.PrefetchScalarGridSpec(
+            num_scalar_prefetch=1,
+            grid=(1,),
+            in_specs=[pl.BlockSpec(shape, lambda i, p: (0, 0))] * 16,
+            out_specs=pl.BlockSpec((16,) + shape, lambda i, p: (0, 0, 0)),
+        ),
+        out_shape=jax.ShapeDtypeStruct((16,) + shape, BF),
+        name="assemble",
+    )(place, *pieces)
+
+
 def pick(arr, index, axis):
     return lax.dynamic_index_in_dim(arr, index, axis, keepdims=False)
 
@@ -206,41 +359,67 @@
 
 
 def dp_gather(shard):
-    count = lax.axis_size("dp")
-    if count != 16:
-        return lax.all_gather(shard, "dp", axis=0, tiled=False)
+    return lax.all_gather(shard, "dp", axis=0, tiled=False)
+
+
+def dp_scatter(parts):
+    flat = parts.reshape((-1,) + parts.shape[2:])
+    return lax.psum_scatter(flat, "dp", scatter_dimension=0, tiled=True).astype(F32)
+
+
+def dp_place():
     index = lax.axis_index("dp")
-    z, x, core = index // 4, (index // 2) % 2, index % 2
-    got = [shard] + [
-        lax.ppermute(shard, "dp", [(j, (j - 4 * s) % 16) for j in range(16)]) for s in (1, 2, 3)
-    ]
-    ring = jnp.stack(got + got[:3])
-    column = lax.dynamic_slice_in_dim(ring, (4 - z) % 4, 4, 0)
-    over_x = lax.ppermute(column, "dp", [(j, j ^ 2) for j in range(16)])
-    plane = ordered(column, over_x, x, 1)
-    over_core = lax.ppermute(plane, "dp", [(j, j ^ 1) for j in range(16)])
-    return ordered(plane, over_core, core, 2).reshape((16,) + shard.shape)
-
-
-def dp_scatter(parts):
-    count = lax.axis_size("dp")
-    if count != 16:
-        flat = parts.reshape((-1,) + parts.shape[2:])
-        return lax.psum_scatter(flat, "dp", scatter_dimension=0, tiled=True).astype(F32)
-    index = lax.axis_index("dp")
-    z, x, core = index // 4, (index // 2) % 2, index % 2
+    return index // 4, (index // 2) % 2, index % 2
+
+
+def to_core(arr):
+    return lax.ppermute(arr, "dp", [(j, j ^ 1) for j in range(16)])
+
+
+def to_x(arr):
+    return lax.ppermute(arr, "dp", [(j, j ^ 2) for j in range(16)])
+
+
+def to_z(arr, s):
+    return lax.ppermute(arr, "dp", [(j, (j + 4 * s) % 16) for j in range(16)])
+
+
+def gather_z(shard):
+    return [shard] + [to_z(shard, 4 - s) for s in (1, 2, 3)]
+
+
+def gather_rest(line):
+    plane = line + [to_x(piece) for piece in line]
+    return plane + [to_core(piece) for piece in plane]
+
+
+def sum_core(parts):
+    core = dp_place()[2]
     cube = parts.reshape((4, 2, 2) + parts.shape[1:])
-    got = lax.ppermute(pick(cube, 1 - core, 2), "dp", [(j, j ^ 1) for j in range(16)])
-    square = (pick(cube, core, 2).astype(F32) + got.astype(F32)).astype(BF)
-    got = lax.ppermute(pick(square, 1 - x, 1), "dp", [(j, j ^ 2) for j in range(16)])
-    line = (pick(square, x, 1).astype(F32) + got.astype(F32)).astype(BF)
-    total = pick(line, z, 0).astype(F32)
-    for s in (1, 2, 3):
-        got = lax.ppermute(
-            pick(line, (z + s) % 4, 0), "dp", [(j, (j + 4 * s) % 16) for j in range(16)]
-        )
-        total = total + got.astype(F32)
+    return pick(cube, core, 2), to_core(pick(cube, 1 - core, 2))
+
+
+def sum_x(kept, got):
+    x = dp_place()[1]
+    square = (kept.astype(F32) + got.astype(F32)).astype(BF)
+    return pick(square, x, 1), to_x(pick(square, 1 - x, 1))
+
+
+def sum_z(kept, got):
+    z = dp_place()[0]
+    line = (kept.astype(F32) + got.astype(F32)).astype(BF)
+    return pick(line, z, 0), [to_z(pick(line, (z + s) % 4, 0), s) for s in (1, 2, 3)]
+
+
+def sum_end(kept, got):
+    total = kept.astype(F32)
+    for term in got:
+        total = total + term.astype(F32)
     return total
+
+
+def after(value, *others):
+    return lax.optimization_barrier((value,) + tuple(others))[0]
 
 
 def seq_swap(arr):
@@ -484,10 +663,158 @@
     )
 
 
+def body_fast(
+    tokens, lengths, attn_gain, w_query, w_key, w_value, query_gain, key_gain, w_out,
+    ffn_gain, w_gate, w_up, w_down, cotangent,
+):
+    seq_n, dp_n = 2, 16
+    rank = lax.axis_index("seq")
+    dp_rank = lax.axis_index("dp")
+    place = jnp.stack(dp_place()).astype(jnp.int32)
+    own, width = tokens.shape
+    length = own * seq_n
+    q_w, kv_w = H * HD // seq_n, KV * HD // seq_n
+    ff_dp = w_down.shape[0]
+    ff_w = ff_dp // seq_n
+    ff = ff_w * dp_n
+    d_dp = w_query.shape[0]
+    gain_a = attn_gain.astype(F32)[:, None]
+    gain_f = ffn_gain.astype(F32)[:, None]
+    per = query_gain.shape[0]
+
+    packed = ff_prep(rank, w_gate, w_up, w_down, gain_f)
+    ff_full = lax.all_gather(packed, "dp", axis=0, tiled=False)
+
+    def my_cols(w, n):
+        return lax.dynamic_slice_in_dim(w, rank * n, n, 1)
+
+    qkv_part = jnp.concatenate(
+        [my_cols(w_query, q_w), my_cols(w_key, kv_w), my_cols(w_value, kv_w)], axis=1
+    )
+    qkv_part = (qkv_part.astype(F32) * gain_a).astype(BF)
+    gains = jnp.concatenate([query_gain, key_gain])
+    gains = jnp.pad(gains[None, :], ((0, 7), (0, qkv_part.shape[1] - gains.shape[0])))
+    qkv_line = gather_z(jnp.concatenate([qkv_part, gains], axis=0))
+    xhat_a, inv_a = unit_rms(tokens)
+    low_own = xhat_a.astype(BF)
+    low_other = seq_swap(low_own)
+    got = assemble(place, gather_rest(qkv_line))
+    qkv_full = got[:, :d_dp].reshape(width, -1)
+    gain_q = got[:, d_dp, :per].reshape(-1).astype(F32)
+    gain_k = got[:, d_dp, per : 2 * per].reshape(-1).astype(F32)
+    out_pieces = gather_rest(gather_z(after(w_out, *qkv_line)))
+    g_own = cotangent.astype(BF)
+    g_other = seq_swap(after(g_own, low_other))
+
+    low_a = ordered(low_own, low_other, rank, 0).reshape(length, width)
+    lin = dot(qkv_full, low_a, 0, 1)
+    q_lin, k_lin = lin[:q_w], lin[q_w : q_w + kv_w]
+    values = lin[q_w + kv_w :].astype(BF)
+    freqs = ROPE_BASE ** (-(jnp.arange(HD // 2, dtype=F32) * (2.0 / HD)))
+    angles = freqs[:, None] * jnp.arange(length, dtype=jnp.int32).astype(F32)[None, :]
+    cos_tab, sin_tab = jnp.cos(angles), jnp.sin(angles)
+    queries = head_prep(q_lin, gain_q, cos_tab, sin_tab, 1.0 / math.sqrt(HD))
+    keys = head_prep(k_lin, gain_k, cos_tab, sin_tab, 1.0)
+    att_heads, lse = attn_fwd(queries, keys, values, None)
+    attended = heads_to_tokens(att_heads)
+    out_full = assemble(place, out_pieces).reshape(H * HD, width)
+    resid = tokens + dot(attended, out_full, 0, 0)
+
+    xhat_f, inv_f = unit_rms(resid)
+    x_own = xhat_f.astype(BF)
+    x_other = seq_swap(x_own)
+    sizes = (dp_n, d_dp, ff_w)
+    *wide, dx_own, out_own = ffn_core(x_own, g_own, ff_full, None, 0, *sizes)
+    *wide, dx_other, out_other = ffn_core(x_other, g_other, ff_full, wide, 1, *sizes)
+    hidden, d_gate, d_up = wide
+    dx_got = seq_swap(dx_other.astype(BF))
+    x_all = jnp.concatenate([x_own, x_other], axis=0)
+    g_all = jnp.concatenate([g_own, g_other], axis=0)
+    g1 = sum_core(dot(x_all, d_gate, 0, 0).astype(BF).reshape(dp_n, d_dp, ff))
+    u1 = sum_core(dot(x_all, d_up, 0, 0).astype(BF).reshape(dp_n, d_dp, ff))
+    g2 = sum_x(*g1)
+    d1 = sum_core(dot(after(hidden, g1[1]), g_all, 0, 0).astype(BF).reshape(dp_n, ff_w, width))
+    u2 = sum_x(*u1)
+
+    d_ffn = dx_own + dx_got.astype(F32)
+    d_resid = cotangent + unit_rms_back(after(d_ffn, u1[1]), xhat_f, inv_f)
+    r_low = d_resid.astype(BF)
+    d_att = tokens_to_heads(dot(out_full, r_low, 1, 1).astype(BF))
+    o1 = sum_core(dot(attended, r_low, 1, 0).astype(BF).reshape(dp_n, d_dp, width))
+    g3 = sum_z(*g2)
+    d2 = sum_x(*d1)
+    d_att = after(d_att, g2[1], d1[1], o1[1])
+    d_q, d_k, d_v = attn_bwd(queries, keys, values, d_att, att_heads, lse, None)
+    u3 = sum_z(*u2)
+    o2 = sum_x(*o1)
+    d_q = after(d_q, u2[1])
+    d_q, d_gq = head_prep_back(d_q, q_lin, gain_q, cos_tab, sin_tab)
+    d_k, d_gk = head_prep_back(d_k, k_lin, gain_k, cos_tab, sin_tab)
+    d_lin = jnp.concatenate([d_q, d_k, d_v], axis=0)
+    d_lin = after(d_lin, *g3[1])
+    d_norm = dot(d_lin, qkv_full, 0, 1)
+    other = lax.dynamic_slice_in_dim(d_norm, (1 - rank) * own, own, 0)
+    d_norm = lax.dynamic_slice_in_dim(d_norm, rank * own, own, 0)
+    d_norm = d_norm + seq_swap(other.astype(BF)).astype(F32)
+    d_tokens = d_resid + unit_rms_back(d_norm, xhat_a, inv_a)
+
+    d_w_x = dot(low_a, d_lin, 0, 1).astype(BF).reshape(dp_n, d_dp, -1)
+    d_g = jnp.concatenate([d_gq, d_gk]).astype(BF)
+    d_g = jnp.pad(d_g[None, :], ((0, 7), (0, d_w_x.shape[2] - d_g.shape[0])))
+    d_g = jnp.broadcast_to(d_g[None], (dp_n,) + d_g.shape)
+    x1 = sum_core(jnp.concatenate([d_w_x, d_g], axis=1))
+    d3 = sum_z(*d2)
+    x2 = sum_x(*x1)
+    o3 = sum_z(*o2)
+    x3 = sum_z(*x2)
+    block_out = resid + out_own + seq_swap(out_other.astype(BF)).astype(F32)
+
+    def full_ff(shard):
+        both = seq_stack(shard.astype(BF)).reshape(seq_n, d_dp, dp_n, ff_w)
+        return both.transpose(1, 2, 0, 3).reshape(d_dp, dp_n * seq_n * ff_w).astype(F32)
+
+    d_w_g, d_w_u = full_ff(sum_end(*g3)), full_ff(sum_end(*u3))
+    d_w_d = seq_stack(sum_end(*d3).astype(BF)).reshape(ff_dp, width).astype(F32)
+    d_ffn_gain = jnp.sum(w_gate.astype(F32) * d_w_g + w_up.astype(F32) * d_w_u, axis=1)
+    d_w_x = seq_stack(sum_end(*x3).astype(BF)).astype(F32)
+    both = d_w_x[:, :d_dp]
+    join = lambda lo, n: both[:, :, lo : lo + n].transpose(1, 0, 2).reshape(d_dp, seq_n * n)
+    d_w_q, d_w_k, d_w_v = join(0, q_w), join(q_w, kv_w), join(q_w + kv_w, kv_w)
+    d_gains = jnp.sum(d_w_x[:, d_dp, : 2 * HD], axis=0)
+    d_gq = lax.dynamic_slice_in_dim(d_gains, dp_rank * per, per)
+    d_gk = lax.dynamic_slice_in_dim(d_gains, HD + dp_rank * per, per)
+    d_attn_gain = jnp.sum(w_query.astype(F32) * d_w_q, axis=1) + jnp.sum(
+        w_key.astype(F32) * d_w_k + w_value.astype(F32) * d_w_v, axis=1
+    )
+    d_w_o = jnp.sum(seq_stack(sum_end(*o3).astype(BF)).astype(F32), axis=0)
+    return (
+        block_out,
+        d_tokens,
+        d_attn_gain,
+        d_w_q * gain_a,
+        d_w_k * gain_a,
+        d_w_v * gain_a,
+        d_gq,
+        d_gk,
+        d_w_o,
+        d_ffn_gain,
+        d_w_g * gain_f,
+        d_w_u * gain_f,
+        d_w_d,
+    )
+
+
+def body_for(*args):
+    tokens, lengths = args[:2]
+    sizes = (lax.axis_size("dp"), lax.axis_size("seq"))
+    exact = lengths.shape[1] == 1 and tokens.shape[0] * sizes[1] == MINLEN
+    return (body_fast if sizes == (16, 2) and exact else body)(*args)
+
+
 def solution(mesh):
     rows, shard, vec = P(("dp", "seq"), None), P("dp", None), P("dp")
     return jax.shard_map(
-        body,
+        body_for,
         mesh=mesh,
         in_specs=(
             rows, shard, vec, shard, shard, shard, vec, vec, shard, vec, shard, shard, shard, rows,

time: 572 us -> 567 us (level)
  Pallas kernels: 37.5 us -> 108 us
  matrix products: 95.8 us -> 33.7 us
  waiting for transfers between devices: 229 us -> 180 us
  starting transfers between devices: 57.6 us -> 86.9 us
  other arithmetic: 66 us -> 72.4 us
    pallas_call x0 -> x5, Pallas kernels: none -> 70.8 us  [the longest x2 58.7 us: ffn_core(): pl.pallas_call(partial(ffn_core_kernel, 384, fresh), grid=(2,), in_specs=...]
    dot_general x15 -> x9, matrix products: 95.8 us -> 33.7 us  [dot(): lax.dot_general(left, right, (((lc,), (rc,)), ((), ())), preferred_elemen...]
    ppermute x35 -> x55, starting transfers between devices: 39.2 us -> 70.7 us  [the longest x21 50.6 us: to_z(): return lax.ppermute(arr, 'dp', [(j, (j + 4 * s) % 16) for j in range(16)])]
    ppermute x35 -> x55, waiting for transfers between devices: 150 us -> 120 us  [the longest x13 64.5 us: to_x(): return lax.ppermute(arr, 'dp', [(j, j ^ 2) for j in range(16)])]
    ppermute x13, waiting for transfers between devices: 78.3 us -> 50.3 us  [seq_swap(): return lax.ppermute(arr, 'seq', [(0, 1), (1, 0)])]
    all_gather x2 -> x1, waiting for transfers between devices: 0.01 us -> 9.62 us  [body_fast(): ff_full = lax.all_gather(packed, 'dp', axis=0, tiled=False)]
    another operation x16 -> x8, other arithmetic: 12 us -> 3.07 us  [ordered(): return jnp.stack([low_, high], axis=axis)]
    convert_element_type x25, other arithmetic: 19.1 us -> 27.3 us  [the longest x5 8.34 us: sum_x(): square = (kept.astype(F32) + got.astype(F32)).astype(BF)]
  transfers between devices with their start and end apart: 50 -> 69, of which waited for: 22 -> 28; matrix products, arithmetic and copies ran while one was open for 28% -> 23% of each run, Pallas kernels for 7% -> 13%
where the time goes in v2:
time: 567 us; the launch traced here: 557 us
  waiting for transfers between devices  180 us (32%)
  Pallas kernels  108 us (19%)
  starting transfers between devices  86.9 us (15%)
  other arithmetic  72.4 us (13%)
  local copies, waits for them, and re-layouts  60.1 us (11%)
  matrix products  33.7 us (6%)
  between operations  15.8 us (3%)
    ppermute x13, waiting for transfers between devices, to_x(): return lax.ppermute(arr, 'dp', [(j, j ^ 2) for j in range(16)])  64.5 us
    pallas_call x2, Pallas kernels, ffn_core(): pl.pallas_call(partial(ffn_core_kernel, 384, fresh), grid=(2,), in_specs=...  58.7 us
    ppermute x21, waiting for transfers between devices, to_z(): return lax.ppermute(arr, 'dp', [(j, (j + 4 * s) % 16) for j in range(16)])  55.7 us
    ppermute x21, starting transfers between devices, to_z(): return lax.ppermute(arr, 'dp', [(j, (j + 4 * s) % 16) for j in range(16)])  50.6 us
    ppermute x13, waiting for transfers between devices, seq_swap(): return lax.ppermute(arr, 'seq', [(0, 1), (1, 0)])  50.3 us
    dot_general x9, matrix products, dot(): lax.dot_general(left, right, (((lc,), (rc,)), ((), ())), preferred_elemen...  33.7 us
    pallas_call x1, Pallas kernels, attn_bwd(): pl.pallas_call(partial(attn_bwd_kernel, min(256, length), static), grid=(...  22.5 us
    ppermute x13, starting transfers between devices, to_x(): return lax.ppermute(arr, 'dp', [(j, j ^ 2) for j in range(16)])  17.8 us
  transfers between devices with their start and end apart: 69, of which 28 were waited for; matrix products, arithmetic and copies ran while one was open for 23% of the time, Pallas kernels for 13%

profile of v2, /device:TPU:0, one launch (start us, length us, event | category | flops | bytes accessed | tf_op | source)
XLA Modules:
  0.0 557.4 jit_solution(2203278285711832973)
XLA Ops:
  9.3 4.4 ff_prep.1
  15.1 3.0 collective-permute-start.15
  18.4 3.7 collective-permute-start
  24.6 2.2 collective-permute-done.refs_1_
  26.8 15.1 %collective-permute-done.1.refs_2_ = bf16[72,1024]{1,0:T(8,128)(2,1)S(1)} collective-permute-done((bf16[72,1024]{1,0:T(8,128)(2,1)S(1)}, bf16[72,1024]{1,0:T(8,128)(2,1)S(1)}, u32[]{:S(2)}, u32[]{:S(2)}) %collective-permute-start.1) | collective-permute-done | bytes 147488 | tf_op jit(solution)/shard_map/ppermute | solution.py:384
  41.9 2.8 collective-permute-start.4
  47.9 2.0 collective-permute-done.5.refs_6_
  53.9 8.2 %collective-permute-start.18 = (bf16[64,1024]{1,0:T(8,128)(2,1)}, bf16[64,1024]{1,0:T(8,128)(2,1)}, u32[]{:S(2)}, u32[]{:S(2)}) collective-permute-start(bf16[64,1024]{1,0:T(8,128)(2,1)} %refs_0_), channel_id=1, source_target_pairs={{0,16},{2,18},{4,20},{6,22},{8,24},{10,26},{12,28},{14,30},{16,0},... | collective-permute-start | bytes 393224 | tf_op jit(solution)/shard_map/ppermute | solution.py:384
  64.1 3.9 assemble.2
  68.1 3.1 slice.77
  75.3 2.1 copy-done.21
  77.4 2.4 fusion.56
  85.2 14.9 %attn_fwd.1 = (bf16[512,1024]{1,0:T(8,128)(2,1)}, f32[8,1,1024]{2,1,0:T(1,128)}) custom-call(bf16[512,1024]{1,0:T(8,128)(2,1)} %bitcast.261, bf16[256,1024]{1,0:T(8,128)(2,1)} %bitcast.270, bf16[256,1024]{1,0:T(8,128)(2,1)} %slice.126.refs_2_), custom_call_target="tpu_custom_call" | custom-call | flops 2147483648 | bytes 4194304 | tf_op jit(solution)/shard_map/attn_fwd/pallas_call | solution.py:153
  105.6 5.6 collective-permute-done.20.refs_4_
  112.7 4.1 collective-permute-done.21.refs_5_
  116.8 5.6 %collective-permute-done.22.refs_6_ = bf16[64,1024]{1,0:T(8,128)(2,1)S(1)} collective-permute-done((bf16[64,1024]{1,0:T(8,128)(2,1)}, bf16[64,1024]{1,0:T(8,128)(2,1)S(1)}, u32[]{:S(2)}, u32[]{:S(2)}) %collective-permute-start.22) | collective-permute-done | bytes 131104 | tf_op jit(solution)/shard_map/ppermute | solution.py:380
  122.4 5.2 collective-permute-done.23.refs_7_
  128.7 3.1 convert_element_type.420.refs_1_
  131.9 3.8 assemble.3
  135.7 2.0 collective-permute-start.33
  143.5 9.6 %all-gather.3.cloned.1.call-done = bf16[1536,4608]{1,0:T(8,128)(2,1)} async-done(((bf16[96,4608]{1,0:T(8,128)(2,1)}), bf16[1536,4608]{1,0:T(8,128)(2,1)}) %all-gather.3.cloned.1.call-update) | async-done | bytes 14155792 | tf_op jit(solution)/shard_map/all_gather | solution.py:686
  153.1 29.4 %ffn_core.2 = (bf16[1024,2304]{1,0:T(8,128)(2,1)}, bf16[1024,2304]{1,0:T(8,128)(2,1)}, bf16[1024,2304]{1,0:T(8,128)(2,1)}, f32[512,1024]{1,0:T(8,128)}, f32[512,1024]{1,0:T(8,128)}) custom-call(bf16[512,1024]{1,0:T(8,128)(2,1)} %multiply_convert_fusion.refs_0_, bf16[512,1024]{1,0:T(8,128)(2,1)} %convert_element_type.420.refs_1_, ...), custom_call_target="tpu_custom_call" | custom-call | flops 14495514624 | bytes 27525120 | tf_op jit(solution)/shard_map/ffn_core/pallas_call | solution.py:299
  183.8 29.4 %ffn_core.3 = (bf16[1024,2304]{1,0:T(8,128)(2,1)}, bf16[1024,2304]{1,0:T(8,128)(2,1)}, bf16[1024,2304]{1,0:T(8,128)(2,1)}, f32[512,1024]{1,0:T(8,128)}, f32[512,1024]{1,0:T(8,128)}) custom-call(bf16[512,1024]{1,0:T(8,128)(2,1)} %collective-permute-done.32.refs_0_, ...), custom_call_target="tpu_custom_call", output_to_operand_aliasing={{0}: (5, {}), {1}: (6, {}), {2}: (7, {})} | custom-call | flops 14495514624 | bytes 27525120 | tf_op jit(solution)/shard_map/ffn_core/pallas_call | solution.py:299
  213.2 8.5 %convolution_convert_fusion.2 = bf16[1024,2304]{1,0:T(8,128)(2,1)S(1)} fusion(bf16[1024,2304]{1,0:T(8,128)(2,1)} %get-tuple-element.45, bf16[512,1024]{1,0:T(8,128)(2,1)} %collective-permute-done.32.refs_0_, bf16[512,1024]{1,0:T(8,128)(2,1)} %multiply_convert_fusion.refs_0_), kind=kOutput, calls=%fused_computation.2 | convolution fusion | flops 4838391808 | bytes 11534336 | tf_op jit(solution)/shard_map/dot_general | solution.py:25
  224.6 2.9 convert_element_type.424
  229.1 2.7 convert_element_type.422
  232.2 7.3 %convolution_convert_fusion.1 = bf16[1024,2304]{1,0:T(8,128)(2,1)S(1)} fusion(bf16[1024,2304]{1,0:T(8,128)(2,1)S(1)} %copy-done.14, bf16[512,1024]{1,0:T(8,128)(2,1)} %collective-permute-done.32.refs_0_, bf16[512,1024]{1,0:T(8,128)(2,1)} %multiply_convert_fusion.refs_0_), kind=kOutput, calls=%fused_computation.1 | convolution fusion | flops 4838391808 | bytes 11534336 | tf_op jit(solution)/shard_map/dot_general | solution.py:25
  244.1 9.8 %collective-permute-done.35 = bf16[512,1024]{1,0:T(8,128)(2,1)} collective-permute-done((bf16[512,1024]{1,0:T(8,128)(2,1)}, bf16[512,1024]{1,0:T(8,128)(2,1)}, u32[]{:S(2)}, u32[]{:S(2)}) %collective-permute-start.35) | collective-permute-done | bytes 1048608 | tf_op jit(solution)/shard_map/ppermute | solution.py:426
  253.8 2.3 convert_add_fusion.9
  256.7 19.0 %collective-permute-done.34 = bf16[512,1024]{1,0:T(8,128)(2,1)S(1)} collective-permute-done((bf16[512,1024]{1,0:T(8,128)(2,1)}, bf16[512,1024]{1,0:T(8,128)(2,1)S(1)}, u32[]{:S(2)}, u32[]{:S(2)}) %collective-permute-start.34) | collective-permute-done | bytes 1048608 | tf_op jit(solution)/shard_map/ppermute | solution.py:426
  282.2 5.6 %convolution_convert_fusion = bf16[2304,1024]{1,0:T(8,128)(2,1)S(1)} fusion(bf16[1024,2304]{1,0:T(8,128)(2,1)S(1)} %bitcast.243, bf16[512,1024]{1,0:T(8,128)(2,1)S(1)} %copy-done.28, bf16[512,1024]{1,0:T(8,128)(2,1)S(1)} %copy-done.29), kind=kOutput, calls=%fused_computation | convolution fusion | flops 4838391808 | bytes 11534336 | tf_op jit(solution)/shard_map/dot_general | solution.py:25
  291.2 2.4 fusion.2
  296.5 2.2 fusion.1
  300.0 9.1 %collective-permute-done.37 = bf16[512,512]{1,0:T(8,128)(2,1)S(1)} collective-permute-done((bf16[512,512]{1,0:T(8,128)(2,1)S(1)}, bf16[512,512]{1,0:T(8,128)(2,1)S(1)}, u32[]{:S(2)}, u32[]{:S(2)}) %collective-permute-start.37) | collective-permute-done | bytes 524320 | tf_op jit(solution)/shard_map/ppermute | solution.py:426
  312.3 10.3 %collective-permute-done.39 = bf16[4,64,2304]{2,1,0:T(8,128)(2,1)S(1)} collective-permute-done((bf16[4,64,2304]{2,1,0:T(8,128)(2,1)S(1)}, bf16[4,64,2304]{2,1,0:T(8,128)(2,1)S(1)}, u32[]{:S(2)}, u32[]{:S(2)}) %collective-permute-start.39) | collective-permute-done | bytes 1179680 | tf_op jit(solution)/shard_map/ppermute | solution.py:380
  323.0 2.3 collective-permute-start.44
  325.3 22.5 %collective-permute-done.42 = bf16[4,64,2304]{2,1,0:T(8,128)(2,1)S(1)} collective-permute-done((bf16[4,64,2304]{2,1,0:T(8,128)(2,1)S(1)}, bf16[4,64,2304]{2,1,0:T(8,128)(2,1)S(1)}, u32[]{:S(2)}, u32[]{:S(2)}) %collective-permute-start.42) | collective-permute-done | bytes 1179680 | tf_op jit(solution)/shard_map/ppermute | solution.py:380
  351.5 12.9 %collective-permute-done.45 = bf16[64,2304]{1,0:T(8,128)(2,1)S(1)} collective-permute-done((bf16[64,2304]{1,0:T(8,128)(2,1)S(1)}, bf16[64,2304]{1,0:T(8,128)(2,1)S(1)}, u32[]{:S(2)}, u32[]{:S(2)}) %collective-permute-start.45) | collective-permute-done | bytes 294944 | tf_op jit(solution)/shard_map/ppermute | solution.py:384
  366.0 5.4 collective-permute-start.54
  371.3 7.5 %collective-permute-done.60 = bf16[64,2304]{1,0:T(8,128)(2,1)S(1)} collective-permute-done((bf16[64,2304]{1,0:T(8,128)(2,1)S(1)}, bf16[64,2304]{1,0:T(8,128)(2,1)S(1)}, u32[]{:S(2)}, u32[]{:S(2)}) %collective-permute-start.60) | collective-permute-done | bytes 294944 | tf_op jit(solution)/shard_map/ppermute | solution.py:384
  379.8 7.9 %collective-permute-start.56 = (bf16[64,1024]{1,0:T(8,128)(2,1)S(1)}, bf16[64,1024]{1,0:T(8,128)(2,1)S(1)}, u32[]{:S(2)}, u32[]{:S(2)}) collective-permute-start(bf16[64,1024]{1,0:T(8,128)(2,1)S(1)} %get-tuple-element.107), channel_id=1, source_target_pairs={{0,24},{2,26},{4,28},{6,30},{8,0},{10,2},{12,4},{14,6},{16,8},{18,... | collective-permute-start | bytes 393224 | tf_op jit(solution)/shard_map/ppermute | solution.py:384
  394.5 3.0 stack.100
  397.5 4.0 stack.101
  401.5 5.1 convert_bitcast_fusion.1
  406.6 3.7 reshape.337
  412.2 4.0 stack.102
  416.2 4.0 stack.103
  420.2 5.4 convert_bitcast_fusion
  425.6 4.4 reshape.340
  430.0 22.5 %attn_bwd.1 = (bf16[512,1024]{1,0:T(8,128)(2,1)}, bf16[256,1024]{1,0:T(8,128)(2,1)}, bf16[256,1024]{1,0:T(8,128)(2,1)}) custom-call(bf16[512,1024]{1,0:T(8,128)(2,1)} %bitcast.262, bf16[256,1024]{1,0:T(8,128)(2,1)} %bitcast.271, bf16[256,1024]{1,0:T(8,128)(2,1)} %slice.126.refs_2_, bf16[512,1024]{1,0:T(8,128)(2,1)} %pad_maximum_fusion.7.refs_3_, ...), custom_call_target="tpu_custom_call" | custom-call | flops 5368709120 | bytes 7340032 | tf_op jit(solution)/shard_map/attn_bwd/pallas_call | solution.py:177
  461.5 3.7 convolution_convert_fusion.3
  465.2 2.4 fusion.57
  470.3 2.9 fusion
  479.3 2.4 broadcast_multiply_fusion
  483.4 7.2 %collective-permute-done.46 = bf16[512,1024]{1,0:T(8,128)(2,1)} collective-permute-done((bf16[512,1024]{1,0:T(8,128)(2,1)}, bf16[512,1024]{1,0:T(8,128)(2,1)}, u32[]{:S(2)}, u32[]{:S(2)}) %collective-permute-start.46) | collective-permute-done | bytes 1048608 | tf_op jit(solution)/shard_map/ppermute | solution.py:426
  492.4 6.4 %collective-permute-done.63 = bf16[4,144,1024]{2,1,0:T(8,128)(2,1)} collective-permute-done((bf16[4,144,1024]{2,1,0:T(8,128)(2,1)}, bf16[4,144,1024]{2,1,0:T(8,128)(2,1)}, u32[]{:S(2)}, u32[]{:S(2)}) %collective-permute-start.63) | collective-permute-done | bytes 1179680 | tf_op jit(solution)/shard_map/ppermute | solution.py:380
  500.6 2.7 collective-permute-start.64
  503.3 3.0 collective-permute-start.65
  508.8 3.2 multiply_add_fusion
  513.7 7.6 %collective-permute-done.65 = bf16[144,1024]{1,0:T(8,128)(2,1)S(1)} collective-permute-done((bf16[144,1024]{1,0:T(8,128)(2,1)S(1)}, bf16[144,1024]{1,0:T(8,128)(2,1)S(1)}, u32[]{:S(2)}, u32[]{:S(2)}) %collective-permute-start.65) | collective-permute-done | bytes 294944 | tf_op jit(solution)/shard_map/ppermute | solution.py:384
  523.6 8.4 %collective-permute-start.49 = (bf16[72,1024]{1,0:T(8,128)(2,1)S(1)}, bf16[72,1024]{1,0:T(8,128)(2,1)S(1)}, u32[]{:S(2)}, u32[]{:S(2)}) collective-permute-start(bf16[72,1024]{1,0:T(8,128)(2,1)S(1)} %get-tuple-element.103), channel_id=1, source_target_pairs={{0,8},{2,10},{4,12},{6,14},{8,16},{10,18},{12,20},{14,22},{16,24},... | collective-permute-start | bytes 442376 | tf_op jit(solution)/shard_map/ppermute | solution.py:384
  532.0 2.4 collective-permute-start.51
  536.2 4.9 collective-permute-done.50
  543.0 4.0 collective-permute-done.52
  (389 shorter events, 118.2 us)
Async XLA Ops:
  7.2 145.9 %all-gather.3.cloned.1.call-start = ((), (), s32[]{:S(2)}) async-start(), calls=%async_computation | async-start | bytes 15040512 | tf_op jit(solution)/shard_map/all_gather | solution.py:686
  15.1 59.6 %collective-permute-start.15 = (bf16[512,1024]{1,0:T(8,128)(2,1)}, bf16[512,1024]{1,0:T(8,128)(2,1)S(1)}, u32[]{:S(2)}, u32[]{:S(2)}) collective-permute-start(bf16[512,1024]{1,0:T(8,128)(2,1)} %multiply_convert_fusion.1), channel_id=1, source_target_pairs={{0,1},{1,0},{2,3},{3,2},{4,5},{5,4},{6,7},{7,6},{8,9},{9,8},{10,11... | collective-permute-start | bytes 3145736 | tf_op jit(solution)/shard_map/ppermute | solution.py:426
  18.4 8.4 %collective-permute-start = (bf16[72,1024]{1,0:T(8,128)(2,1)S(1)}, bf16[72,1024]{1,0:T(8,128)(2,1)S(1)}, u32[]{:S(2)}, u32[]{:S(2)}) collective-permute-start(bf16[72,1024]{1,0:T(8,128)(2,1)S(1)} %fusion.42.refs_0_), channel_id=1, source_target_pairs={{0,24},{2,26},{4,28},{6,30},{8,0},{10,2},{12,4},{14,6},{16,8},{18,... | collective-permute-start | bytes 442376 | tf_op jit(solution)/shard_map/ppermute | solution.py:384
  22.1 19.8 %collective-permute-start.1 = (bf16[72,1024]{1,0:T(8,128)(2,1)S(1)}, bf16[72,1024]{1,0:T(8,128)(2,1)S(1)}, u32[]{:S(2)}, u32[]{:S(2)}) collective-permute-start(bf16[72,1024]{1,0:T(8,128)(2,1)S(1)} %fusion.42.refs_0_), channel_id=1, source_target_pairs={{0,16},{2,18},{4,20},{6,22},{8,24},{10,26},{12,28},{14,30},{16,0},... | collective-permute-start | bytes 442376 | tf_op jit(solution)/shard_map/ppermute | solution.py:384
  22.1 22.6 %collective-permute-start.2 = (bf16[72,1024]{1,0:T(8,128)(2,1)S(1)}, bf16[72,1024]{1,0:T(8,128)(2,1)S(1)}, u32[]{:S(2)}, u32[]{:S(2)}) collective-permute-start(bf16[72,1024]{1,0:T(8,128)(2,1)S(1)} %fusion.42.refs_0_), channel_id=1, source_target_pairs={{0,8},{2,10},{4,12},{6,14},{8,16},{10,18},{12,20},{14,22},{16,24},... | collective-permute-start | bytes 442376 | tf_op jit(solution)/shard_map/ppermute | solution.py:384
  23.1 21.6 %collective-permute-start.3 = (bf16[72,1024]{1,0:T(8,128)(2,1)S(1)}, bf16[72,1024]{1,0:T(8,128)(2,1)}, u32[]{:S(2)}, u32[]{:S(2)}) collective-permute-start(bf16[72,1024]{1,0:T(8,128)(2,1)S(1)} %fusion.42.refs_0_), channel_id=1, source_target_pairs={{0,4},{2,6},{4,0},{6,2},{8,12},{10,14},{12,8},{14,10},{16,20},{18,... | collective-permute-start | bytes 442376 | tf_op jit(solution)/shard_map/ppermute | solution.py:380
  26.8 19.9 %collective-permute-start.7 = (bf16[72,1024]{1,0:T(8,128)(2,1)S(1)}, bf16[72,1024]{1,0:T(8,128)(2,1)S(1)}, u32[]{:S(2)}, u32[]{:S(2)}) collective-permute-start(bf16[72,1024]{1,0:T(8,128)(2,1)S(1)} %fusion.42.refs_0_), channel_id=1, source_target_pairs={{0,2},{2,0},{4,6},{6,4},{8,10},{10,8},{12,14},{14,12},{16,18},{18,... | collective-permute-start | bytes 442376 | tf_op jit(solution)/shard_map/ppermute | solution.py:376
  41.9 6.0 %collective-permute-start.4 = (bf16[72,1024]{1,0:T(8,128)(2,1)S(1)}, bf16[72,1024]{1,0:T(8,128)(2,1)}, u32[]{:S(2)}, u32[]{:S(2)}) collective-permute-start(bf16[72,1024]{1,0:T(8,128)(2,1)S(1)} %collective-permute-done.refs_1_), channel_id=1, source_target_pairs={{0,4},{2,6},{4,0},{6,2},{8,12},{10,14},{12,8},{14,10},{16,20},{18,... | collective-permute-start | bytes 442376 | tf_op jit(solution)/shard_map/ppermute | solution.py:380
  44.6 5.2 collective-permute-start.5
  44.7 6.7 %collective-permute-start.6 = (bf16[72,1024]{1,0:T(8,128)(2,1)S(1)}, bf16[72,1024]{1,0:T(8,128)(2,1)}, u32[]{:S(2)}, u32[]{:S(2)}) collective-permute-start(bf16[72,1024]{1,0:T(8,128)(2,1)S(1)} %collective-permute-done.2.refs_3_), channel_id=1, source_target_pairs={{0,4},{2,6},{4,0},{6,2},{8,12},{10,14},{12,8},{14,10},{16,20},{18,... | collective-permute-start | bytes 442376 | tf_op jit(solution)/shard_map/ppermute | solution.py:380
  46.7 4.8 collective-permute-start.10
  47.9 4.1 collective-permute-start.8
  52.0 10.2 %collective-permute-start.13 = (bf16[72,1024]{1,0:T(8,128)(2,1)}, bf16[72,1024]{1,0:T(8,128)(2,1)}, u32[]{:S(2)}, u32[]{:S(2)}) collective-permute-start(bf16[72,1024]{1,0:T(8,128)(2,1)} %collective-permute-done.5.refs_6_), channel_id=1, source_target_pairs={{0,2},{2,0},{4,6},{6,4},{8,10},{10,8},{12,14},{14,12},{16,18},{18,... | collective-permute-start | bytes 442376 | tf_op jit(solution)/shard_map/ppermute | solution.py:376
  52.1 12.1 %collective-permute-start.14 = (bf16[72,1024]{1,0:T(8,128)(2,1)}, bf16[72,1024]{1,0:T(8,128)(2,1)}, u32[]{:S(2)}, u32[]{:S(2)}) collective-permute-start(bf16[72,1024]{1,0:T(8,128)(2,1)} %collective-permute-done.6.refs_7_), channel_id=1, source_target_pairs={{0,2},{2,0},{4,6},{6,4},{8,10},{10,8},{12,14},{14,12},{16,18},{18,... | collective-permute-start | bytes 442376 | tf_op jit(solution)/shard_map/ppermute | solution.py:376
  53.9 49.6 %collective-permute-start.17 = (bf16[64,1024]{1,0:T(8,128)(2,1)}, bf16[64,1024]{1,0:T(8,128)(2,1)S(1)}, u32[]{:S(2)}, u32[]{:S(2)}) collective-permute-start(bf16[64,1024]{1,0:T(8,128)(2,1)} %refs_0_), channel_id=1, source_target_pairs={{0,24},{2,26},{4,28},{6,30},{8,0},{10,2},{12,4},{14,6},{16,8},{18,... | collective-permute-start | bytes 393224 | tf_op jit(solution)/shard_map/ppermute | solution.py:384
  53.9 49.6 %collective-permute-start.18 = (bf16[64,1024]{1,0:T(8,128)(2,1)}, bf16[64,1024]{1,0:T(8,128)(2,1)}, u32[]{:S(2)}, u32[]{:S(2)}) collective-permute-start(bf16[64,1024]{1,0:T(8,128)(2,1)} %refs_0_), channel_id=1, source_target_pairs={{0,16},{2,18},{4,20},{6,22},{8,24},{10,26},{12,28},{14,30},{16,0},... | collective-permute-start | bytes 393224 | tf_op jit(solution)/shard_map/ppermute | solution.py:384
  62.2 41.9 %collective-permute-start.19 = (bf16[64,1024]{1,0:T(8,128)(2,1)}, bf16[64,1024]{1,0:T(8,128)(2,1)}, u32[]{:S(2)}, u32[]{:S(2)}) collective-permute-start(bf16[64,1024]{1,0:T(8,128)(2,1)} %refs_0_), channel_id=1, source_target_pairs={{0,8},{2,10},{4,12},{6,14},{8,16},{10,18},{12,20},{14,22},{16,24},... | collective-permute-start | bytes 393224 | tf_op jit(solution)/shard_map/ppermute | solution.py:384
  102.0 35.7 %collective-permute-start.16 = (bf16[512,512]{1,0:T(8,128)(2,1)}, bf16[512,512]{1,0:T(8,128)(2,1)}, u32[]{:S(2)}, u32[]{:S(2)}) collective-permute-start(bf16[512,512]{1,0:T(8,128)(2,1)} %constant_dynamic-slice_fusion.3), channel_id=1, source_target_pairs={{0,1},{1,0},{2,3},{3,2},{4,5},{5,4},{6,7},{7,6},{8,9},{9,8},{10,11... | collective-permute-start | bytes 1572872 | tf_op jit(solution)/shard_map/ppermute | solution.py:426
  102.0 9.2 %collective-permute-start.20 = (bf16[64,1024]{1,0:T(8,128)(2,1)S(1)}, bf16[64,1024]{1,0:T(8,128)(2,1)S(1)}, u32[]{:S(2)}, u32[]{:S(2)}) collective-permute-start(bf16[64,1024]{1,0:T(8,128)(2,1)S(1)} %copy-done.50), channel_id=1, source_target_pairs={{0,4},{2,6},{4,0},{6,2},{8,12},{10,14},{12,8},{14,10},{16,20},{18,... | collective-permute-start | bytes 393224 | tf_op jit(solution)/shard_map/ppermute | solution.py:380
  103.5 9.2 %collective-permute-start.24 = (bf16[64,1024]{1,0:T(8,128)(2,1)S(1)}, bf16[64,1024]{1,0:T(8,128)(2,1)S(1)}, u32[]{:S(2)}, u32[]{:S(2)}) collective-permute-start(bf16[64,1024]{1,0:T(8,128)(2,1)S(1)} %copy-done.50), channel_id=1, source_target_pairs={{0,2},{2,0},{4,6},{6,4},{8,10},{10,8},{12,14},{14,12},{16,18},{18,... | collective-permute-start | bytes 393224 | tf_op jit(solution)/shard_map/ppermute | solution.py:376
  103.5 13.3 %collective-permute-start.21 = (bf16[64,1024]{1,0:T(8,128)(2,1)S(1)}, bf16[64,1024]{1,0:T(8,128)(2,1)S(1)}, u32[]{:S(2)}, u32[]{:S(2)}) collective-permute-start(bf16[64,1024]{1,0:T(8,128)(2,1)S(1)} %collective-permute-done.17.refs_1_), channel_id=1, source_target_pairs={{0,4},{2,6},{4,0},{6,2},{8,12},{10,14},{12,8},{14,10},{16,20},{18,... | collective-permute-start | bytes 393224 | tf_op jit(solution)/shard_map/ppermute | solution.py:380
  104.1 18.3 %collective-permute-start.22 = (bf16[64,1024]{1,0:T(8,128)(2,1)}, bf16[64,1024]{1,0:T(8,128)(2,1)S(1)}, u32[]{:S(2)}, u32[]{:S(2)}) collective-permute-start(bf16[64,1024]{1,0:T(8,128)(2,1)} %collective-permute-done.18.refs_2_), channel_id=1, source_target_pairs={{0,4},{2,6},{4,0},{6,2},{8,12},{10,14},{12,8},{14,10},{16,20},{18,... | collective-permute-start | bytes 393224 | tf_op jit(solution)/shard_map/ppermute | solution.py:380
  111.2 16.4 %collective-permute-start.23 = (bf16[64,1024]{1,0:T(8,128)(2,1)}, bf16[64,1024]{1,0:T(8,128)(2,1)S(1)}, u32[]{:S(2)}, u32[]{:S(2)}) collective-permute-start(bf16[64,1024]{1,0:T(8,128)(2,1)} %collective-permute-done.19.refs_3_), channel_id=1, source_target_pairs={{0,4},{2,6},{4,0},{6,2},{8,12},{10,14},{12,8},{14,10},{16,20},{18,... | collective-permute-start | bytes 393224 | tf_op jit(solution)/shard_map/ppermute | solution.py:380
  112.7 15.0 %collective-permute-start.25 = (bf16[64,1024]{1,0:T(8,128)(2,1)S(1)}, bf16[64,1024]{1,0:T(8,128)(2,1)S(1)}, u32[]{:S(2)}, u32[]{:S(2)}) collective-permute-start(bf16[64,1024]{1,0:T(8,128)(2,1)S(1)} %collective-permute-done.17.refs_1_), channel_id=1, source_target_pairs={{0,2},{2,0},{4,6},{6,4},{8,10},{10,8},{12,14},{14,12},{16,18},{18,... | collective-permute-start | bytes 393224 | tf_op jit(solution)/shard_map/ppermute | solution.py:376
  116.8 11.3 %collective-permute-start.26 = (bf16[64,1024]{1,0:T(8,128)(2,1)}, bf16[64,1024]{1,0:T(8,128)(2,1)S(1)}, u32[]{:S(2)}, u32[]{:S(2)}) collective-permute-start(bf16[64,1024]{1,0:T(8,128)(2,1)} %collective-permute-done.18.refs_2_), channel_id=1, source_target_pairs={{0,2},{2,0},{4,6},{6,4},{8,10},{10,8},{12,14},{14,12},{16,18},{18,... | collective-permute-start | bytes 393224 | tf_op jit(solution)/shard_map/ppermute | solution.py:376
  122.4 5.8 %collective-permute-start.27 = (bf16[64,1024]{1,0:T(8,128)(2,1)}, bf16[64,1024]{1,0:T(8,128)(2,1)S(1)}, u32[]{:S(2)}, u32[]{:S(2)}) collective-permute-start(bf16[64,1024]{1,0:T(8,128)(2,1)} %collective-permute-done.19.refs_3_), channel_id=1, source_target_pairs={{0,2},{2,0},{4,6},{6,4},{8,10},{10,8},{12,14},{14,12},{16,18},{18,... | collective-permute-start | bytes 393224 | tf_op jit(solution)/shard_map/ppermute | solution.py:376
  127.6 4.1 collective-permute-start.28
  127.7 4.1 collective-permute-start.29
  135.7 46.8 %collective-permute-start.33 = (bf16[512,1024]{1,0:T(8,128)(2,1)}, bf16[512,1024]{1,0:T(8,128)(2,1)S(1)}, u32[]{:S(2)}, u32[]{:S(2)}) collective-permute-start(bf16[512,1024]{1,0:T(8,128)(2,1)} %convert_element_type.420.refs_1_), channel_id=1, source_target_pairs={{0,1},{1,0},{2,3},{3,2},{4,5},{5,4},{6,7},{7,6},{8,9},{9,8},{10,11... | collective-permute-start | bytes 3145736 | tf_op jit(solution)/shard_map/ppermute | solution.py:426
  143.1 40.7 %collective-permute-start.32 = (bf16[512,1024]{1,0:T(8,128)(2,1)}, bf16[512,1024]{1,0:T(8,128)(2,1)}, u32[]{:S(2)}, u32[]{:S(2)}) collective-permute-start(bf16[512,1024]{1,0:T(8,128)(2,1)} %multiply_convert_fusion.refs_0_), channel_id=1, source_target_pairs={{0,1},{1,0},{2,3},{3,2},{4,5},{5,4},{6,7},{7,6},{8,9},{9,8},{10,11... | collective-permute-start | bytes 3145736 | tf_op jit(solution)/shard_map/ppermute | solution.py:426
  224.6 31.6 %collective-permute-start.36 = (bf16[4,2,64,2304]{3,2,1,0:T(8,128)(2,1)}, bf16[4,2,64,2304]{3,2,1,0:T(8,128)(2,1)}, u32[]{:S(2)}, u32[]{:S(2)}) collective-permute-start(bf16[4,2,64,2304]{3,2,1,0:T(8,128)(2,1)} %dynamic-slice_bitcast_fusion.1), channel_id=1, source_target_pairs={{0,2},{2,0},{4,6},{6,4},{8,10},{10,8},{12,14},{14,12},{16,18},{18,... | collective-permute-start | bytes 7077896 | tf_op jit(solution)/shard_map/ppermute | solution.py:376
  227.5 26.3 %collective-permute-start.35 = (bf16[512,1024]{1,0:T(8,128)(2,1)}, bf16[512,1024]{1,0:T(8,128)(2,1)}, u32[]{:S(2)}, u32[]{:S(2)}) collective-permute-start(bf16[512,1024]{1,0:T(8,128)(2,1)} %convert_element_type.424), channel_id=1, source_target_pairs={{0,1},{1,0},{2,3},{3,2},{4,5},{5,4},{6,7},{7,6},{8,9},{9,8},{10,11... | collective-permute-start | bytes 3145736 | tf_op jit(solution)/shard_map/ppermute | solution.py:426
  231.8 43.9 %collective-permute-start.34 = (bf16[512,1024]{1,0:T(8,128)(2,1)}, bf16[512,1024]{1,0:T(8,128)(2,1)S(1)}, u32[]{:S(2)}, u32[]{:S(2)}) collective-permute-start(bf16[512,1024]{1,0:T(8,128)(2,1)} %convert_element_type.422), channel_id=1, source_target_pairs={{0,1},{1,0},{2,3},{3,2},{4,5},{5,4},{6,7},{7,6},{8,9},{9,8},{10,11... | collective-permute-start | bytes 3145736 | tf_op jit(solution)/shard_map/ppermute | solution.py:426
  242.8 38.6 %collective-permute-start.38 = (bf16[4,2,64,2304]{3,2,0,1:T(8,128)(2,1)}, bf16[4,2,64,2304]{3,2,0,1:T(8,128)(2,1)}, u32[]{:S(2)}, u32[]{:S(2)}) collective-permute-start(bf16[4,2,64,2304]{3,2,0,1:T(8,128)(2,1)} %bitcast.233), channel_id=1, source_target_pairs={{0,2},{2,0},{4,6},{6,4},{8,10},{10,8},{12,14},{14,12},{16,18},{18,... | collective-permute-start | bytes 7077896 | tf_op jit(solution)/shard_map/ppermute | solution.py:376
  291.0 139.0 %collective-permute-start.40 = (bf16[4,2,144,1024]{3,2,1,0:T(8,128)(2,1)}, bf16[4,2,144,1024]{3,2,1,0:T(8,128)(2,1)}, u32[]{:S(2)}, u32[]{:S(2)}) collective-permute-start(bf16[4,2,144,1024]{3,2,1,0:T(8,128)(2,1)} %dynamic-slice_bitcast_fusion), channel_id=1, source_target_pairs={{0,2},{2,0},{4,6},{6,4},{8,10},{10,8},{12,14},{14,12},{16,18},{18,... | collective-permute-start | bytes 7077896 | tf_op jit(solution)/shard_map/ppermute | solution.py:376
  293.7 28.9 %collective-permute-start.39 = (bf16[4,64,2304]{2,1,0:T(8,128)(2,1)S(1)}, bf16[4,64,2304]{2,1,0:T(8,128)(2,1)S(1)}, u32[]{:S(2)}, u32[]{:S(2)}) collective-permute-start(bf16[4,64,2304]{2,1,0:T(8,128)(2,1)S(1)} %dynamic-slice_bitcast_fusion.4), channel_id=1, source_target_pairs={{0,4},{2,6},{4,0},{6,2},{8,12},{10,14},{12,8},{14,10},{16,20},{18,... | collective-permute-start | bytes 3538952 | tf_op jit(solution)/shard_map/ppermute | solution.py:380
  294.6 15.9 %collective-permute-start.41 = (bf16[4,2,64,1024]{3,2,1,0:T(8,128)(2,1)S(1)}, bf16[4,2,64,1024]{3,2,1,0:T(8,128)(2,1)S(1)}, u32[]{:S(2)}, u32[]{:S(2)}) collective-permute-start(bf16[4,2,64,1024]{3,2,1,0:T(8,128)(2,1)S(1)} %dynamic-slice_bitcast_fusion.5), channel_id=1, source_target_pairs={{0,2},{2,0},{4,6},{6,4},{8,10},{10,8},{12,14},{14,12},{16,18},{18,... | collective-permute-start | bytes 3145736 | tf_op jit(solution)/shard_map/ppermute | solution.py:376
  294.8 14.4 %collective-permute-start.37 = (bf16[512,512]{1,0:T(8,128)(2,1)S(1)}, bf16[512,512]{1,0:T(8,128)(2,1)S(1)}, u32[]{:S(2)}, u32[]{:S(2)}) collective-permute-start(bf16[512,512]{1,0:T(8,128)(2,1)S(1)} %constant_dynamic-slice_fusion.2), channel_id=1, source_target_pairs={{0,1},{1,0},{2,3},{3,2},{4,5},{5,4},{6,7},{7,6},{8,9},{9,8},{10,11... | collective-permute-start | bytes 1572872 | tf_op jit(solution)/shard_map/ppermute | solution.py:426
  298.8 49.1 %collective-permute-start.42 = (bf16[4,64,2304]{2,1,0:T(8,128)(2,1)S(1)}, bf16[4,64,2304]{2,1,0:T(8,128)(2,1)S(1)}, u32[]{:S(2)}, u32[]{:S(2)}) collective-permute-start(bf16[4,64,2304]{2,1,0:T(8,128)(2,1)S(1)} %dynamic-slice_bitcast_fusion.3), channel_id=1, source_target_pairs={{0,4},{2,6},{4,0},{6,2},{8,12},{10,14},{12,8},{14,10},{16,20},{18,... | collective-permute-start | bytes 3538952 | tf_op jit(solution)/shard_map/ppermute | solution.py:380
  311.0 53.5 %collective-permute-start.53 = (bf16[4,64,1024]{2,1,0:T(8,128)(2,1)S(1)}, bf16[4,64,1024]{2,1,0:T(8,128)(2,1)S(1)}, u32[]{:S(2)}, u32[]{:S(2)}) collective-permute-start(bf16[4,64,1024]{2,1,0:T(8,128)(2,1)S(1)} %dynamic-slice_bitcast_fusion.7), channel_id=1, source_target_pairs={{0,4},{2,6},{4,0},{6,2},{8,12},{10,14},{12,8},{14,10},{16,20},{18,... | collective-permute-start | bytes 1572872 | tf_op jit(solution)/shard_map/ppermute | solution.py:380
  323.0 27.0 %collective-permute-start.43 = (bf16[64,2304]{1,0:T(8,128)(2,1)S(1)}, bf16[64,2304]{1,0:T(8,128)(2,1)S(1)}, u32[]{:S(2)}, u32[]{:S(2)}) collective-permute-start(bf16[64,2304]{1,0:T(8,128)(2,1)S(1)} %get-tuple-element.94), channel_id=1, source_target_pairs={{0,8},{2,10},{4,12},{6,14},{8,16},{10,18},{12,20},{14,22},{16,24},... | collective-permute-start | bytes 884744 | tf_op jit(solution)/shard_map/ppermute | solution.py:384
  323.0 27.3 %collective-permute-start.44 = (bf16[64,2304]{1,0:T(8,128)(2,1)S(1)}, bf16[64,2304]{1,0:T(8,128)(2,1)S(1)}, u32[]{:S(2)}, u32[]{:S(2)}) collective-permute-start(bf16[64,2304]{1,0:T(8,128)(2,1)S(1)} %get-tuple-element.93), channel_id=1, source_target_pairs={{0,16},{2,18},{4,20},{6,22},{8,24},{10,26},{12,28},{14,30},{16,0},... | collective-permute-start | bytes 884744 | tf_op jit(solution)/shard_map/ppermute | solution.py:384
  347.9 16.5 %collective-permute-start.45 = (bf16[64,2304]{1,0:T(8,128)(2,1)S(1)}, bf16[64,2304]{1,0:T(8,128)(2,1)S(1)}, u32[]{:S(2)}, u32[]{:S(2)}) collective-permute-start(bf16[64,2304]{1,0:T(8,128)(2,1)S(1)} %get-tuple-element.92), channel_id=1, source_target_pairs={{0,24},{2,26},{4,28},{6,30},{8,0},{10,2},{12,4},{14,6},{16,8},{18,... | collective-permute-start | bytes 884744 | tf_op jit(solution)/shard_map/ppermute | solution.py:384
  350.0 16.0 %collective-permute-start.59 = (bf16[64,2304]{1,0:T(8,128)(2,1)S(1)}, bf16[64,2304]{1,0:T(8,128)(2,1)S(1)}, u32[]{:S(2)}, u32[]{:S(2)}) collective-permute-start(bf16[64,2304]{1,0:T(8,128)(2,1)S(1)} %get-tuple-element.89), channel_id=1, source_target_pairs={{0,8},{2,10},{4,12},{6,14},{8,16},{10,18},{12,20},{14,22},{16,24},... | collective-permute-start | bytes 884744 | tf_op jit(solution)/shard_map/ppermute | solution.py:384
  350.3 28.5 %collective-permute-start.60 = (bf16[64,2304]{1,0:T(8,128)(2,1)S(1)}, bf16[64,2304]{1,0:T(8,128)(2,1)S(1)}, u32[]{:S(2)}, u32[]{:S(2)}) collective-permute-start(bf16[64,2304]{1,0:T(8,128)(2,1)S(1)} %get-tuple-element.91), channel_id=1, source_target_pairs={{0,16},{2,18},{4,20},{6,22},{8,24},{10,26},{12,28},{14,30},{16,0},... | collective-permute-start | bytes 884744 | tf_op jit(solution)/shard_map/ppermute | solution.py:384
  364.4 15.4 %collective-permute-start.61 = (bf16[64,2304]{1,0:T(8,128)(2,1)S(1)}, bf16[64,2304]{1,0:T(8,128)(2,1)S(1)}, u32[]{:S(2)}, u32[]{:S(2)}) collective-permute-start(bf16[64,2304]{1,0:T(8,128)(2,1)S(1)} %get-tuple-element.90), channel_id=1, source_target_pairs={{0,24},{2,26},{4,28},{6,30},{8,0},{10,2},{12,4},{14,6},{16,8},{18,... | collective-permute-start | bytes 884744 | tf_op jit(solution)/shard_map/ppermute | solution.py:384
  364.6 29.1 %collective-permute-start.58 = (bf16[64,2304]{1,0:T(8,128)(2,1)S(1)}, bf16[64,2304]{1,0:T(8,128)(2,1)S(1)}, u32[]{:S(2)}, u32[]{:S(2)}) collective-permute-start(bf16[64,2304]{1,0:T(8,128)(2,1)S(1)} %fusion.32), channel_id=1, source_target_pairs={{0,1},{1,0},{2,3},{3,2},{4,5},{5,4},{6,7},{7,6},{8,9},{9,8},{10,11... | collective-permute-start | bytes 884744 | tf_op jit(solution)/shard_map/ppermute | solution.py:426
  366.0 22.6 %collective-permute-start.54 = (bf16[64,1024]{1,0:T(8,128)(2,1)S(1)}, bf16[64,1024]{1,0:T(8,128)(2,1)S(1)}, u32[]{:S(2)}, u32[]{:S(2)}) collective-permute-start(bf16[64,1024]{1,0:T(8,128)(2,1)S(1)} %get-tuple-element.106), channel_id=1, source_target_pairs={{0,8},{2,10},{4,12},{6,14},{8,16},{10,18},{12,20},{14,22},{16,24},... | collective-permute-start | bytes 393224 | tf_op jit(solution)/shard_map/ppermute | solution.py:384
  378.8 11.5 %collective-permute-start.55 = (bf16[64,1024]{1,0:T(8,128)(2,1)S(1)}, bf16[64,1024]{1,0:T(8,128)(2,1)S(1)}, u32[]{:S(2)}, u32[]{:S(2)}) collective-permute-start(bf16[64,1024]{1,0:T(8,128)(2,1)S(1)} %get-tuple-element.108), channel_id=1, source_target_pairs={{0,16},{2,18},{4,20},{6,22},{8,24},{10,26},{12,28},{14,30},{16,0},... | collective-permute-start | bytes 393224 | tf_op jit(solution)/shard_map/ppermute | solution.py:384
  379.8 11.4 %collective-permute-start.56 = (bf16[64,1024]{1,0:T(8,128)(2,1)S(1)}, bf16[64,1024]{1,0:T(8,128)(2,1)S(1)}, u32[]{:S(2)}, u32[]{:S(2)}) collective-permute-start(bf16[64,1024]{1,0:T(8,128)(2,1)S(1)} %get-tuple-element.107), channel_id=1, source_target_pairs={{0,24},{2,26},{4,28},{6,30},{8,0},{10,2},{12,4},{14,6},{16,8},{18,... | collective-permute-start | bytes 393224 | tf_op jit(solution)/shard_map/ppermute | solution.py:384
  388.6 21.7 %collective-permute-start.62 = (bf16[64,2304]{1,0:T(8,128)(2,1)}, bf16[64,2304]{1,0:T(8,128)(2,1)}, u32[]{:S(2)}, u32[]{:S(2)}) collective-permute-start(bf16[64,2304]{1,0:T(8,128)(2,1)} %fusion.29), channel_id=1, source_target_pairs={{0,1},{1,0},{2,3},{3,2},{4,5},{5,4},{6,7},{7,6},{8,9},{9,8},{10,11... | collective-permute-start | bytes 884744 | tf_op jit(solution)/shard_map/ppermute | solution.py:426
  391.9 89.7 %collective-permute-start.57 = (bf16[64,1024]{1,0:T(8,128)(2,1)}, bf16[64,1024]{1,0:T(8,128)(2,1)}, u32[]{:S(2)}, u32[]{:S(2)}) collective-permute-start(bf16[64,1024]{1,0:T(8,128)(2,1)} %fusion.41), channel_id=1, source_target_pairs={{0,1},{1,0},{2,3},{3,2},{4,5},{5,4},{6,7},{7,6},{8,9},{9,8},{10,11... | collective-permute-start | bytes 393224 | tf_op jit(solution)/shard_map/ppermute | solution.py:426
  470.0 20.6 %collective-permute-start.46 = (bf16[512,1024]{1,0:T(8,128)(2,1)}, bf16[512,1024]{1,0:T(8,128)(2,1)}, u32[]{:S(2)}, u32[]{:S(2)}) collective-permute-start(bf16[512,1024]{1,0:T(8,128)(2,1)} %dynamic-slice_convert_fusion), channel_id=1, source_target_pairs={{0,1},{1,0},{2,3},{3,2},{4,5},{5,4},{6,7},{7,6},{8,9},{9,8},{10,11... | collective-permute-start | bytes 3145736 | tf_op jit(solution)/shard_map/ppermute | solution.py:426
  475.6 23.2 %collective-permute-start.63 = (bf16[4,144,1024]{2,1,0:T(8,128)(2,1)}, bf16[4,144,1024]{2,1,0:T(8,128)(2,1)}, u32[]{:S(2)}, u32[]{:S(2)}) collective-permute-start(bf16[4,144,1024]{2,1,0:T(8,128)(2,1)} %dynamic-slice_bitcast_fusion.2), channel_id=1, source_target_pairs={{0,4},{2,6},{4,0},{6,2},{8,12},{10,14},{12,8},{14,10},{16,20},{18,... | collective-permute-start | bytes 3538952 | tf_op jit(solution)/shard_map/ppermute | solution.py:380
  479.0 27.7 %collective-permute-start.47 = (bf16[4,2,72,1024]{3,2,0,1:T(8,128)(2,1)S(1)}, bf16[4,2,72,1024]{3,2,0,1:T(8,128)(2,1)S(1)}, u32[]{:S(2)}, u32[]{:S(2)}) collective-permute-start(bf16[4,2,72,1024]{3,2,0,1:T(8,128)(2,1)S(1)} %fusion.16), channel_id=1, source_target_pairs={{0,2},{2,0},{4,6},{6,4},{8,10},{10,8},{12,14},{14,12},{16,18},{18,... | collective-permute-start | bytes 3538952 | tf_op jit(solution)/shard_map/ppermute | solution.py:376
  500.6 13.1 %collective-permute-start.64 = (bf16[144,1024]{1,0:T(8,128)(2,1)S(1)}, bf16[144,1024]{1,0:T(8,128)(2,1)S(1)}, u32[]{:S(2)}, u32[]{:S(2)}) collective-permute-start(bf16[144,1024]{1,0:T(8,128)(2,1)S(1)} %get-tuple-element.83), channel_id=1, source_target_pairs={{0,8},{2,10},{4,12},{6,14},{8,16},{10,18},{12,20},{14,22},{16,24},... | collective-permute-start | bytes 884744 | tf_op jit(solution)/shard_map/ppermute | solution.py:384
  503.3 17.9 %collective-permute-start.65 = (bf16[144,1024]{1,0:T(8,128)(2,1)S(1)}, bf16[144,1024]{1,0:T(8,128)(2,1)S(1)}, u32[]{:S(2)}, u32[]{:S(2)}) collective-permute-start(bf16[144,1024]{1,0:T(8,128)(2,1)S(1)} %get-tuple-element.85), channel_id=1, source_target_pairs={{0,16},{2,18},{4,20},{6,22},{8,24},{10,26},{12,28},{14,30},{16,0},... | collective-permute-start | bytes 884744 | tf_op jit(solution)/shard_map/ppermute | solution.py:384
  506.4 14.9 %collective-permute-start.66 = (bf16[144,1024]{1,0:T(8,128)(2,1)S(1)}, bf16[144,1024]{1,0:T(8,128)(2,1)S(1)}, u32[]{:S(2)}, u32[]{:S(2)}) collective-permute-start(bf16[144,1024]{1,0:T(8,128)(2,1)S(1)} %get-tuple-element.84), channel_id=1, source_target_pairs={{0,24},{2,26},{4,28},{6,30},{8,0},{10,2},{12,4},{14,6},{16,8},{18,... | collective-permute-start | bytes 884744 | tf_op jit(solution)/shard_map/ppermute | solution.py:384
  507.2 16.1 %collective-permute-start.48 = (bf16[4,72,1024]{2,1,0:T(8,128)(2,1)S(1)}, bf16[4,72,1024]{2,1,0:T(8,128)(2,1)S(1)}, u32[]{:S(2)}, u32[]{:S(2)}) collective-permute-start(bf16[4,72,1024]{2,1,0:T(8,128)(2,1)S(1)} %dynamic-slice_bitcast_fusion.6), channel_id=1, source_target_pairs={{0,4},{2,6},{4,0},{6,2},{8,12},{10,14},{12,8},{14,10},{16,20},{18,... | collective-permute-start | bytes 1769480 | tf_op jit(solution)/shard_map/ppermute | solution.py:380
  521.5 12.9 %collective-permute-start.67 = (bf16[144,1024]{1,0:T(8,128)(2,1)S(1)}, bf16[144,1024]{1,0:T(8,128)(2,1)S(1)}, u32[]{:S(2)}, u32[]{:S(2)}) collective-permute-start(bf16[144,1024]{1,0:T(8,128)(2,1)S(1)} %fusion.26), channel_id=1, source_target_pairs={{0,1},{1,0},{2,3},{3,2},{4,5},{5,4},{6,7},{7,6},{8,9},{9,8},{10,11... | collective-permute-start | bytes 884744 | tf_op jit(solution)/shard_map/ppermute | solution.py:426
  523.6 12.7 %collective-permute-start.49 = (bf16[72,1024]{1,0:T(8,128)(2,1)S(1)}, bf16[72,1024]{1,0:T(8,128)(2,1)S(1)}, u32[]{:S(2)}, u32[]{:S(2)}) collective-permute-start(bf16[72,1024]{1,0:T(8,128)(2,1)S(1)} %get-tuple-element.103), channel_id=1, source_target_pairs={{0,8},{2,10},{4,12},{6,14},{8,16},{10,18},{12,20},{14,22},{16,24},... | collective-permute-start | bytes 442376 | tf_op jit(solution)/shard_map/ppermute | solution.py:384
  532.0 9.2 %collective-permute-start.50 = (bf16[72,1024]{1,0:T(8,128)(2,1)S(1)}, bf16[72,1024]{1,0:T(8,128)(2,1)S(1)}, u32[]{:S(2)}, u32[]{:S(2)}) collective-permute-start(bf16[72,1024]{1,0:T(8,128)(2,1)S(1)} %get-tuple-element.105), channel_id=1, source_target_pairs={{0,16},{2,18},{4,20},{6,22},{8,24},{10,26},{12,28},{14,30},{16,0},... | collective-permute-start | bytes 442376 | tf_op jit(solution)/shard_map/ppermute | solution.py:384
  532.0 9.4 %collective-permute-start.51 = (bf16[72,1024]{1,0:T(8,128)(2,1)S(1)}, bf16[72,1024]{1,0:T(8,128)(2,1)S(1)}, u32[]{:S(2)}, u32[]{:S(2)}) collective-permute-start(bf16[72,1024]{1,0:T(8,128)(2,1)S(1)} %get-tuple-element.104), channel_id=1, source_target_pairs={{0,24},{2,26},{4,28},{6,30},{8,0},{10,2},{12,4},{14,6},{16,8},{18,... | collective-permute-start | bytes 442376 | tf_op jit(solution)/shard_map/ppermute | solution.py:384
  541.4 5.5 collective-permute-start.52
  (87 other events, 566.9 us)
Sparse Core Ops, SparseCore 0:
  13.8 139.2 all-gather.2
